TPU v7x, 32 devices: a whole 2x2x4 slice. The times are simulated.
32 devices in a mesh: bx: 8 (over y, x, core), by: 4 (over z).
Axes of the slice: x: 2, y: 2, z: 4, core: 2. Of those that a mesh axis runs over, the one named last changes fastest.
Arguments:
- photon_data: float32 [6, 512, 128, 128], P(None, 'bx', 'by'), may hold values from 0 to 1, as said below
- block_counts: int32 [512, 128], P('bx', 'by'), may hold values from 1 to 128
- gather_offsets: float32 [3, 131072], P(None, ('bx', 'by')), may hold values from 0 to 1, as said below
- gather_blocks: int32 [4, 131072], P(None, ('bx', 'by')), may hold values from 0 to 65535, as said below
- albedo: float32 [3, 131072], P(None, ('bx', 'by')), may hold values from 0.1 to 1
- gather_pixels: int32 [131072], P(('bx', 'by')), may hold values from 0 to 65535, as said below
- tile_slot: int32 [256], replicated, may hold values from 0 to 255, as said below
Outputs:
- film: float32 [3, 256, 256], P(None, ('bx', 'by'))
Inputs may be any that keep to these rules, and one draw needn't show every extreme that they name: `photon_data`: per point and channel in cell units: entries 0 to 2 are a position in [0, 1), entries 3 to 5 a positive power. `gather_offsets`: each coordinate lies in [0, 1). `gather_blocks`: entry 0 is the point's own cell, inside the brick of the device that holds the point; the 4 entries are the four different cells of a 2 x 2 square of cells (periodic) that contains it. `gather_pixels`: in the rows of one device, at most 384 gather points lie in tiles whose slots s share s // 8; in every draw some such owner group receives exactly 384 from every device. `tile_slot`: A permutation of 0 to 255.
All inputs are finite; a program needn't handle non-finite values.
Results may differ from a plain program's by a relative error of at most 0.0003.
Values sent between devices are 32-bit elements; how exact they have to be, the bound alone decides.
A program may use at most 512 MiB of HBM per device.

v0:
```python
import functools

import jax
import jax.numpy as jnp
from jax import lax
from jax.experimental import pallas as pl
from jax.experimental.pallas import tpu as pltpu
from jax.sharding import PartitionSpec as P

TILE_PIX = 256
INV_RADIUS_SQ = 4.0
FAR = 1.0e4
LANES = 128
MESH = pl.DeviceIdType.MESH
NT = (((1,), (1,)), ((), ()))
PITCH = LANES + 1


def halo_kernel(nx, ny, cx, cy, first, photons, recv, send, send_sem, recv_sem, edge_sem):
    ix, iy = lax.axis_index("bx"), lax.axis_index("by")
    right, left = lax.rem(ix + 1, nx), lax.rem(ix + nx - 1, nx)
    up, down = lax.rem(iy + 1, ny), lax.rem(iy + ny - 1, ny)
    peers = [
        (right, iy, 0, cy),
        (left, iy, cy, cy),
        (ix, up, 2 * cy, cx),
        (ix, down, 2 * cy + cx, cx),
        (right, up, 2 * cy + 2 * cx, 8),
        (right, down, 2 * cy + 2 * cx + 8, 8),
        (left, up, 2 * cy + 2 * cx + 16, 8),
        (left, down, 2 * cy + 2 * cx + 24, 8),
    ]
    every, tail, head = pl.ds(0, cy), pl.ds(cy - 8, 8), pl.ds(0, 8)
    wide = pl.ds(0, cx)
    cuts = [
        (cx - 1, every), (0, every), (wide, cy - 1), (wide, 0),
        (cx - 1, tail), (cx - 1, head), (0, tail), (0, head),
    ]
    edges = []
    for n, (x, y) in enumerate(cuts):
        part = pl.ds(peers[n][2], peers[n][3])
        edges.append(
            pltpu.make_async_copy(
                photons.at[pl.ds(1, 5), x, y], send.at[pl.ds(1, 5), part], edge_sem.at[2 * n]
            )
        )
        edges.append(
            pltpu.make_async_copy(first.at[x, y], send.at[0, part], edge_sem.at[2 * n + 1])
        )
    for n in (2, 3, 0, 1, 4, 5, 6, 7):
        edges[2 * n].start()
        edges[2 * n + 1].start()
    barrier = pltpu.get_barrier_semaphore()
    for px, py, _, _ in peers:
        pl.semaphore_signal(barrier, inc=1, device_id=(px, py), device_id_type=MESH)
    pl.semaphore_wait(barrier, len(peers))
    copies = []
    for n, (px, py, first, rows) in enumerate(peers):
        part = pl.ds(first, rows)
        copies.append(
            pltpu.make_async_remote_copy(
                src_ref=send.at[:, part],
                dst_ref=recv.at[:, part],
                send_sem=send_sem.at[n],
                recv_sem=recv_sem.at[n],
                device_id=(px, py),
                device_id_type=MESH,
            )
        )
    for n in (2, 3, 0, 1, 4, 5, 6, 7):
        edges[2 * n].wait()
        edges[2 * n + 1].wait()
        copies[n].start()
    for copy in copies:
        copy.wait()


def exchange_halo(first, photons, nx, ny, cx, cy):
    shape = (6, 2 * cy + 2 * cx + 32, photons.shape[3])
    return pl.pallas_call(
        functools.partial(halo_kernel, nx, ny, cx, cy),
        out_shape=jax.ShapeDtypeStruct(shape, jnp.float32),
        in_specs=[pl.BlockSpec(memory_space=pl.ANY)] * 2,
        out_specs=pl.BlockSpec(memory_space=pl.ANY),
        scratch_shapes=[
            pltpu.VMEM(shape, jnp.float32),
            pltpu.SemaphoreType.DMA((8,)),
            pltpu.SemaphoreType.DMA((8,)),
            pltpu.SemaphoreType.DMA((16,)),
        ],
        compiler_params=pltpu.CompilerParams(collective_id=0, has_side_effects=True),
        name="halo",
    )(first, photons)


def radiance_kernel(
    cells, rows, owners, cap_rows,
    idx, pts, alb, meta, first, rest, halo, out,
    table, stage, wide, acc, packed, tri, spread, sems,
):
    listed = 4
    points = pts.shape[1]
    fills = [pltpu.make_async_copy(first, table.at[pl.ds(0, cells), 0], sems.at[0])]
    for c in range(1, 6):
        fills.append(pltpu.make_async_copy(rest.at[c], table.at[pl.ds(0, cells), c], sems.at[c]))
    for c in range(6):
        fills.append(
            pltpu.make_async_copy(
                halo.at[c], table.at[pl.ds(cells, rows - cells), c], sems.at[6 + c]
            )
        )
    for fill in fills:
        fill.start()
    a = lax.broadcasted_iota(jnp.int32, (LANES, LANES), 0)
    b = lax.broadcasted_iota(jnp.int32, (LANES, LANES), 1)
    tri[...] = jnp.where(a < b, 1.0, 0.0).astype(jnp.bfloat16)
    a = lax.broadcasted_iota(jnp.int32, spread.shape, 0)
    b = lax.broadcasted_iota(jnp.int32, spread.shape, 1)
    spread[...] = jnp.where(a % 16 == b // LANES, 1.0, 0.0).astype(jnp.bfloat16)
    packed[...] = jnp.zeros_like(packed)
    own_iota = lax.broadcasted_iota(jnp.int32, (owners, LANES), 0)
    cap_iota = lax.broadcasted_iota(jnp.int32, (cap_rows * LANES, LANES), 0).astype(jnp.float32)
    for fill in fills:
        fill.wait()

    def block(blk, carry):
        base = pl.multiple_of(blk * LANES, LANES)
        span = pl.ds(base, LANES)
        value = pts[:, span]
        parts = []
        for _ in range(3):
            high = value.astype(jnp.bfloat16)
            parts.append(high)
            value = value - high.astype(jnp.float32)
        wide[...] = lax.dot_general(
            jnp.concatenate(parts, axis=0), spread[...], (((0,), (0,)), ((), ())),
            preferred_element_type=jnp.float32,
        )
        for p in range(LANES):
            for k in range(listed):
                stage[pl.ds(k * 8 * PITCH + p, 8, stride=PITCH), :] = table[
                    idx[k * points + base + p]
                ]
        for q in range(LANES // 8):
            place = slice(q * 8, q * 8 + 8)

            def column(n):
                return wide[place, n * LANES : (n + 1) * LANES]

            oz = column(8)
            totals = [None] * 3
            for k in range(listed):
                def chan(c):
                    return stage[pl.ds((k * 8 + c) * PITCH + q * 8, 8), :]

                dx = chan(0) - column(k)
                dy = chan(1) - column(4 + k)
                dz = chan(2) - oz
                d2 = dx * dx + dy * dy + dz * dz
                w = jnp.maximum(1.0 - d2 * INV_RADIUS_SQ, 0.0)
                for c in range(3):
                    term = w * chan(3 + c)
                    totals[c] = term if k == 0 else totals[c] + term
            for c in range(3):
                acc[c, place, :] = totals[c]
        own = meta[0:1, span]
        mine = own_iota == own
        hot = jnp.where(mine, 1.0, 0.0)
        before = jnp.dot(hot.astype(jnp.bfloat16), tri[...], preferred_element_type=jnp.float32)
        rank = jnp.sum(jnp.where(mine, before + carry, 0.0), axis=0, keepdims=True)
        values = []
        for c in range(3):
            rad = jnp.sum(acc[c].T, axis=0, keepdims=True) * alb[c : c + 1, span]
            high = rad.astype(jnp.bfloat16).astype(jnp.float32)
            values += [high, rad - high]
        values += [meta[1:2, span].astype(jnp.float32), meta[2:3, span].astype(jnp.float32)]
        left = jnp.concatenate(
            [jnp.where(mine, v, 0.0).astype(jnp.bfloat16) for v in values], axis=0
        )
        right = jnp.where(cap_iota == rank, 1.0, 0.0).astype(jnp.bfloat16)
        packed[...] += lax.dot_general(left, right, NT, preferred_element_type=jnp.float32)
        return carry + jnp.sum(hot, axis=1, keepdims=True)

    lax.fori_loop(0, points // LANES, block, jnp.zeros((owners, 1), jnp.float32))
    pitch = out.shape[0] // owners

    def part(v, j):
        return packed[pl.ds(v * owners, owners), pl.ds(j * LANES, LANES)]

    for j in range(cap_rows):
        for c in range(3):
            out[pl.ds(c * cap_rows + j, owners, stride=pitch), :] = part(2 * c, j) + part(2 * c + 1, j)
        out[pl.ds(3 * cap_rows + j, owners, stride=pitch), :] = part(6, j)
        out[pl.ds(4 * cap_rows + j, owners, stride=pitch), :] = part(7, j)
    for r in range(5 * cap_rows, pitch):
        out[pl.ds(r, owners, stride=pitch), :] = jnp.zeros((owners, LANES), jnp.float32)


def pack_radiance(idx, pts, alb, meta, first, photons, halo, owners, cap_rows):
    cells = first.shape[0]
    rows = cells + halo.shape[1]
    pitch = -(-5 * cap_rows // 8) * 8
    vm = pl.BlockSpec(memory_space=pltpu.VMEM)
    hb = pl.BlockSpec(memory_space=pl.ANY)
    return pl.pallas_call(
        functools.partial(radiance_kernel, cells, rows, owners, cap_rows),
        out_shape=jax.ShapeDtypeStruct((owners * pitch, LANES), jnp.float32),
        in_specs=[pl.BlockSpec(memory_space=pltpu.SMEM), vm, vm, vm, hb, hb, hb],
        out_specs=vm,
        scratch_shapes=[
            pltpu.VMEM((rows, 8, LANES), jnp.float32),
            pltpu.VMEM((4 * 8 * PITCH + 8, LANES), jnp.float32),
            pltpu.VMEM((LANES, 9 * LANES), jnp.float32),
            pltpu.VMEM((3, LANES, LANES), jnp.float32),
            pltpu.VMEM((8 * owners, cap_rows * LANES), jnp.float32),
            pltpu.VMEM((LANES, LANES), jnp.bfloat16),
            pltpu.VMEM((48, 9 * LANES), jnp.bfloat16),
            pltpu.SemaphoreType.DMA((12,)),
        ],
        name="radiance",
    )(idx, pts, alb, meta, first, photons, halo)


def film_kernel(nx, ny, cap_rows, unroll, send, out, recv, send_sem, recv_sem, own_sem):
    count = nx * ny
    ix, iy = lax.axis_index("bx"), lax.axis_index("by")
    me = ix * ny + iy
    barrier = pltpu.get_barrier_semaphore()

    def greet(s, _):
        to = lax.rem(me + s, count)
        pl.semaphore_signal(
            barrier, inc=1, device_id=(to // ny, lax.rem(to, ny)), device_id_type=MESH
        )
        return 0

    lax.fori_loop(1, count, greet, 0)
    own = pltpu.make_async_copy(send.at[me], recv.at[me], own_sem)
    own.start()
    pl.semaphore_wait(barrier, count - 1)

    def copy_to(s):
        to = lax.rem(me + s, count)
        return pltpu.make_async_remote_copy(
            src_ref=send.at[to],
            dst_ref=recv.at[me],
            send_sem=send_sem.at[to],
            recv_sem=recv_sem.at[me],
            device_id=(to // ny, lax.rem(to, ny)),
            device_id_type=MESH,
        )

    def go(s, _):
        copy_to(s).start()
        return 0

    lax.fori_loop(1, count, go, 0)
    own.wait()

    def arrive(s):
        come = lax.rem(me + count - s, count)

        @pl.when(s > 0)
        def _():
            pltpu.make_async_remote_copy(
                src_ref=send.at[come],
                dst_ref=recv.at[come],
                send_sem=send_sem.at[come],
                recv_sem=recv_sem.at[come],
                device_id=(come // ny, lax.rem(come, ny)),
                device_id_type=MESH,
            ).wait_recv()

        return come

    tiles = out.shape[1]
    halves = out.shape[2] // LANES
    high_rows = tiles * halves
    high_iota = lax.broadcasted_iota(jnp.int32, (high_rows, LANES), 0).astype(jnp.float32)
    low_iota = lax.broadcasted_iota(jnp.int32, (LANES, LANES), 0).astype(jnp.float32)

    def add(step, total):
        lefts, rights = [], []
        sources = [arrive(step * unroll + u) for u in range(unroll)]
        for come in sources:
            blk = recv[come]
            for j in range(cap_rows):
                def row(v):
                    r = v * cap_rows + j
                    return blk[r : r + 1]
                here = high_iota == row(3)
                parts = []
                for c in range(3):
                    value = row(c)
                    top = value.astype(jnp.bfloat16).astype(jnp.float32)
                    parts += [jnp.where(here, top, 0.0), jnp.where(here, value - top, 0.0)]
                lefts.append(jnp.concatenate(parts, axis=0).astype(jnp.bfloat16))
                rights.append(jnp.where(low_iota == row(4), 1.0, 0.0).astype(jnp.bfloat16))
        left = jnp.concatenate(lefts, axis=1)
        right = jnp.concatenate(rights, axis=1)
        return total + lax.dot_general(left, right, NT, preferred_element_type=jnp.float32)

    total = lax.fori_loop(
        0, count // unroll, add, jnp.zeros((6 * high_rows, LANES), jnp.float32)
    )
    for c in range(3):
        for h in range(halves):
            at = 2 * c * high_rows + h * tiles
            out[c, :, h * LANES : (h + 1) * LANES] = (
                total[at : at + tiles] + total[at + high_rows : at + high_rows + tiles]
            )

    def sent(s, _):
        copy_to(s).wait_send()
        return 0

    lax.fori_loop(1, count, sent, 0)


def gather_film(send, nx, ny, cap_rows, tiles):
    count = nx * ny
    return pl.pallas_call(
        functools.partial(film_kernel, nx, ny, cap_rows, 4),
        out_shape=jax.ShapeDtypeStruct((3, tiles, TILE_PIX), jnp.float32),
        in_specs=[pl.BlockSpec(memory_space=pltpu.VMEM)],
        out_specs=pl.BlockSpec(memory_space=pltpu.VMEM),
        scratch_shapes=[
            pltpu.VMEM(send.shape, jnp.float32),
            pltpu.SemaphoreType.DMA((count,)),
            pltpu.SemaphoreType.DMA((count,)),
            pltpu.SemaphoreType.DMA,
        ],
        compiler_params=pltpu.CompilerParams(collective_id=1, has_side_effects=True),
        name="film",
    )(send)


def per_device(
    nx, ny, photon_data, block_counts, gather_offsets, gather_blocks, albedo, gather_pixels, tile_slot
):
    cx, cy, slots = photon_data.shape[1:]
    grid_x, grid_y = cx * nx, cy * ny
    points = gather_offsets.shape[1]
    owners = nx * ny
    tiles = tile_slot.shape[0]
    tiles_dev = tiles // owners
    cap_rows = -(-(3 * points // owners) // LANES)

    live = lax.broadcasted_iota(jnp.int32, (cx, cy, slots), 2) < block_counts[:, :, None]
    first = jnp.where(live, photon_data[0], FAR)

    first = lax.optimization_barrier(first)
    halo = exchange_halo(first, photon_data, nx, ny, cx, cy)

    first_x = lax.axis_index("bx") * cx
    first_y = lax.axis_index("by") * cy
    lx = (gather_blocks // grid_y - first_x + 1) % grid_x
    ly = (gather_blocks % grid_y - first_y + 1) % grid_y
    shift_x = (lx - lx[:1]).astype(jnp.float32)
    shift_y = (ly - ly[:1]).astype(jnp.float32)
    cells = cx * cy
    x_out = (lx == 0) | (lx == cx + 1)
    y_out = (ly == 0) | (ly == cy + 1)
    x_far = (lx == cx + 1).astype(jnp.int32)
    y_far = (ly == cy + 1).astype(jnp.int32)
    corner = 2 * cy + 2 * cx + 16 * x_far + 8 * y_far + 7 * (1 - y_far)
    index = jnp.where(
        x_out,
        jnp.where(y_out, cells + corner, cells + x_far * cy + ly - 1),
        jnp.where(y_out, cells + 2 * cy + y_far * cx + lx - 1, (lx - 1) * cy + ly - 1),
    )
    pts = jnp.concatenate(
        [
            gather_offsets[0:1] - shift_x,
            gather_offsets[1:2] - shift_y,
            gather_offsets[2:3],
            jnp.zeros((7, points), jnp.float32),
        ],
        axis=0,
    )
    tile = gather_pixels // TILE_PIX
    matched = tile[:, None] == jnp.arange(tiles, dtype=jnp.int32)[None, :]
    slot = jnp.sum(jnp.where(matched, tile_slot[None, :], 0), axis=1)
    within = gather_pixels % TILE_PIX
    meta = jnp.stack(
        [slot // tiles_dev, (within // LANES) * tiles_dev + slot % tiles_dev, within % LANES]
    )
    packed = pack_radiance(
        index.reshape(-1), pts, albedo, meta, first.reshape(cells, slots),
        photon_data.reshape(6, cells, slots), halo, owners, cap_rows,
    )
    return gather_film(packed.reshape(owners, -1, LANES), nx, ny, cap_rows, tiles_dev)


def solution(mesh):
    both = ("bx", "by")
    in_specs = (
        P(None, "bx", "by", None), P("bx", "by"), P(None, both), P(None, both),
        P(None, both), P(both), P(),
    )
    return jax.shard_map(
        functools.partial(per_device, mesh.shape["bx"], mesh.shape["by"]),
        mesh=mesh, in_specs=in_specs, out_specs=P(None, both, None), check_vma=False,
    )
```

profile of v0, /device:TPU:0, one launch (start us, length us, event | category | flops | bytes accessed | tf_op | source)
XLA Modules:
  0.0 83.0 jit_solution(13372362493702605054)
XLA Ops:
  0.0 0.1 pad.6.clone
  0.1 0.7 add_select_fusion.8
  0.8 2.0 %select_reduce_fusion = s32[4096]{0:T(1024)S(1)} fusion(s32[256]{0:T(256)} %param.13, s32[4096]{0:T(1024)S(1)} %add_select_fusion.8), kind=kLoop, calls=%fused_computation | loop fusion | flops 3141632 | bytes 33792 | tf_op jit(solution)/shard_map/reduce_sum | solution.py:383
  2.8 0.1 and_select_fusion
  2.9 0.8 copy.9
  3.7 0.8 fusion.9
  4.4 0.7 pad_add_fusion.meta
  5.1 1.0 %fusion.15 = (f32[1,4096]{1,0:T(1,128)S(1)}, f32[1,4096]{1,0:T(1,128)S(1)}, f32[1,4096]{1,0:T(1,128)S(1)}) fusion(f32[3,4096]{1,0:T(4,128)} %param.9), kind=kLoop, calls=%fused_computation.58 | loop fusion | bytes 98304 | tf_op jit(solution)/shard_map/slice | solution.py:374
  6.1 1.2 %select_bitcast_fusion = (s32[1,32,4,128]{3,2,1,0:T(4,128)S(1)}, s32[4,4096]{1,0:T(4,128)S(1)}, s32[4,4096]{1,0:T(4,128)S(1)}) fusion(s32[]{:T(128)S(6)} %mul.38, s32[4,4096]{1,0:T(4,128)} %param.10, s32[]{:T(128)S(6)} %mul.39), kind=kLoop, calls=%fused_computation.25 | loop fusion | flops 1228800 | bytes 262152
  7.3 0.6 copy.10
  8.0 0.1 convert_subtract_fusion
  8.0 0.8 maximum_maximum_fusion.pts
  8.8 2.5 %bitcast_select_fusion.first = f32[64,32,128]{2,1,0:T(8,128)} fusion(f32[6,64,32,128]{3,2,1,0:T(8,128)} %photons.1, s32[64,32]{1,0:T(8,128)S(1)} %copy.9), kind=kLoop, calls=%fused_computation.2 | loop fusion | flops 524288 | bytes 2105344 | tf_op jit(solution)/shard_map/jit(_where)/select_n | solution.py:350
  11.4 17.4 %halo.1 = f32[6,224,128]{2,1,0:T(8,128)} custom-call(f32[64,32,128]{2,1,0:T(8,128)} %bitcast_select_fusion.first, f32[6,64,32,128]{3,2,1,0:T(8,128)} %photons.1), custom_call_target="tpu_custom_call" | custom-call | tf_op jit(solution)/shard_map/halo/pallas_call | solution.py:80
  28.7 36.9 %radiance.1 = f32[512,128]{1,0:T(8,128)} custom-call(s32[16384]{0:T(1024)} %bitcast.18, f32[16,4096]{1,0:T(8,128)} %maximum_maximum_fusion.pts, f32[3,4096]{1,0:T(4,128)} %alb.1, s32[3,4096]{1,0:T(4,128)} %pad_add_fusion.meta, f32[2048,128]{1,0:T(8,128)} %bitcast.16, f32[6,2048,128]{2,1,0:T(8,128)} %bitcast.15, f32[6,224,128]{2,1,0:T(8,128)} %halo.1), custom_call_target="tpu_custom_call" | custom-call | tf_op jit(solution)/shard_map/radiance/pallas_call | solution.py:205
  65.7 16.0 %film.1 = f32[3,8,256]{2,1,0:T(8,128)} custom-call(f32[32,16,128]{2,1,0:T(8,128)} %bitcast.17), custom_call_target="tpu_custom_call" | custom-call | tf_op jit(solution)/shard_map/film/pallas_call | solution.py:322
  81.7 1.3 %copy.12 = f32[3,8,256]{2,1,0:T(8,128)} copy(f32[3,8,256]{2,1,0:T(8,128)} %film.1) | data formatting | bytes 49152
  (3 shorter events, 0.0 us)
where the time goes:
time: 83.6 us; the launch traced here: 83 us
  Pallas kernels  70.3 us (84%)
  other arithmetic  8.78 us (11%)
  local copies, waits for them, and re-layouts  3.87 us (5%)
    pallas_call x1, Pallas kernels, pack_radiance(): pl.pallas_call(functools.partial(radiance_kernel, cells, rows, owners, ca...  36.9 us
    pallas_call x1, Pallas kernels, exchange_halo(): pl.pallas_call(functools.partial(halo_kernel, nx, ny, cx, cy), out_shape=...  17.4 us
    pallas_call x1, Pallas kernels, gather_film(): pl.pallas_call(functools.partial(film_kernel, nx, ny, cap_rows, 4), out_s...  16 us
    unnamed x3, local copies, waits for them, and re-layouts  2.77 us
    select_n x1, other arithmetic, per_device(): first = jnp.where(live, photon_data[0], FAR)  2.54 us
    reduce_sum x1, other arithmetic, per_device(): slot = jnp.sum(jnp.where(matched, tile_slot[None, :], 0), axis=1)  1.96 us

commit v1 on v0

v1 whole, which is shorter than its diff:
```python
import functools

import jax
import jax.numpy as jnp
from jax import lax
from jax.experimental import pallas as pl
from jax.experimental.pallas import tpu as pltpu
from jax.sharding import PartitionSpec as P

TILE_PIX = 256
INV_RADIUS_SQ = 4.0
FAR = 1.0e4
LANES = 128
ROWS = 8
CHANNELS = 6
MESH = pl.DeviceIdType.MESH
NT = (((1,), (1,)), ((), ()))
PITCH = 9
GROUP = 4 * ROWS * PITCH
SQUARE = ((0, 0), (0, 1), (1, 0), (1, 1))


def split_by(value, size):
    if size & (size - 1) == 0:
        return value >> (size.bit_length() - 1), value & (size - 1)
    return lax.div(value, size), lax.rem(value, size)


def whole_kernel(
    nx, ny, cap_rows, tiles_dev,
    photons, counts, offsets, blocks, albedo, pixels, tile_slot, out,
    table, edge_x, edge_y, stage_a, stage_b, wide_a, wide_b, acc_a, acc_b,
    spread, tri, count_row, count_col, points_v, base_v, base_s, owner_v, pixel_v,
    packed, send, recv,
    fill_sem, edge_sem, base_sem, halo_send, halo_recv, send_sem, recv_sem,
):
    cx, cy = photons.shape[1], photons.shape[2]
    pitch_y = cy + 2
    grid_x, grid_y = cx * nx, cy * ny
    points = offsets.shape[1]
    steps = points // LANES
    owners = nx * ny
    pitch = send.shape[1]
    used = 4 * cap_rows
    ix, iy = lax.axis_index("bx"), lax.axis_index("by")
    me = ix * ny + iy

    edges = []
    for c in range(CHANNELS):
        for s, x in enumerate((cx - 1, 0)):
            edges.append(
                pltpu.make_async_copy(
                    photons.at[c, x], edge_x.at[s, :, c], edge_sem.at[len(edges)]
                )
            )
        for s, y in enumerate((cy - 1, 0)):
            edges.append(
                pltpu.make_async_copy(
                    photons.at[c, :, y], edge_y.at[s, :, c], edge_sem.at[len(edges)]
                )
            )
    for edge in edges:
        edge.start()
    fills = [
        pltpu.make_async_copy(
            photons.at[c], table.at[pl.ds(1, cx), pl.ds(1, cy), c], fill_sem.at[c]
        )
        for c in range(CHANNELS)
    ]
    for fill in fills:
        fill.start()
    barrier = pltpu.get_barrier_semaphore()

    def greet(s, _):
        to = lax.rem(me + s, owners)
        pl.semaphore_signal(
            barrier, inc=1, device_id=(to // ny, lax.rem(to, ny)), device_id_type=MESH
        )
        return 0

    lax.fori_loop(1, owners, greet, 0)

    count_row[...] = counts[...].astype(jnp.float32)
    square = jnp.concatenate(
        [count_row[...], jnp.zeros((cy, LANES - cx), jnp.float32)], axis=1
    )
    square = jnp.concatenate([square, jnp.zeros((LANES - cy, LANES), jnp.float32)], axis=0)
    count_col[...] = square.T
    lane = lax.broadcasted_iota(jnp.int32, (ROWS, LANES), 1).astype(jnp.float32)

    def hide(ref, first, column):
        rows = column.shape[0]
        for r in range(0, rows, ROWS):
            place = pl.ds(first + r * ROWS, ROWS, stride=ROWS)
            ref[place, :] = jnp.where(lane < column[r : r + ROWS], ref[place, :], FAR)

    for edge in edges:
        edge.wait()
    flat_x = edge_x.reshape(2 * cy * ROWS, LANES)
    flat_y = edge_y.reshape(2 * cx * ROWS, LANES)
    for s, x in enumerate((cx - 1, 0)):
        hide(flat_x, s * cy * ROWS, count_row[:, x : x + 1])
    for s, y in enumerate((cy - 1, 0)):
        hide(flat_y, s * cx * ROWS, count_col[0:cx, y : y + 1])
    pl.semaphore_wait(barrier, owners - 1)

    right, left = lax.rem(ix + 1, nx), lax.rem(ix + nx - 1, nx)
    up, down = lax.rem(iy + 1, ny), lax.rem(iy + ny - 1, ny)
    data = pl.ds(0, CHANNELS)
    wide_x, wide_y = pl.ds(1, cx), pl.ds(1, cy)
    parts = [
        (edge_y.at[0, :, data], table.at[wide_x, 0, data], ix, up),
        (edge_y.at[1, :, data], table.at[wide_x, cy + 1, data], ix, down),
        (edge_x.at[0, :, data], table.at[0, wide_y, data], right, iy),
        (edge_x.at[1, :, data], table.at[cx + 1, wide_y, data], left, iy),
        (edge_x.at[0, cy - 1, data], table.at[0, 0, data], right, up),
        (edge_x.at[0, 0, data], table.at[0, cy + 1, data], right, down),
        (edge_x.at[1, cy - 1, data], table.at[cx + 1, 0, data], left, up),
        (edge_x.at[1, 0, data], table.at[cx + 1, cy + 1, data], left, down),
    ]
    halos = [
        pltpu.make_async_remote_copy(
            src_ref=src, dst_ref=dst, send_sem=halo_send.at[n], recv_sem=halo_recv.at[n],
            device_id=(px, py), device_id_type=MESH,
        )
        for n, (src, dst, px, py) in enumerate(parts)
    ]
    for halo in halos:
        halo.start()

    cell_x, cell_y = split_by(blocks[...], grid_y)

    def local(cell, first, size):
        t = cell - first + 1
        t = jnp.where(t < 0, t + size, t)
        return jnp.where(t >= size, t - size, t)

    lx, ly = local(cell_x, ix * cx, grid_x), local(cell_y, iy * cy, grid_y)
    low_x, low_y = jnp.min(lx, axis=0, keepdims=True), jnp.min(ly, axis=0, keepdims=True)
    base = jnp.minimum(low_x, cx) * pitch_y + jnp.minimum(low_y, cy)
    for j in range(steps):
        base_v[j : j + 1, :] = base[:, j * LANES : (j + 1) * LANES]
    to_scalar = pltpu.make_async_copy(base_v, base_s, base_sem)
    to_scalar.start()
    points_v[...] = jnp.zeros_like(points_v)
    points_v[0:1, :] = offsets[0:1, :] + (lx[0:1] - low_x).astype(jnp.float32)
    points_v[1:2, :] = offsets[1:2, :] + (ly[0:1] - low_y).astype(jnp.float32)
    points_v[2:3, :] = offsets[2:3, :]

    tile, within = split_by(pixels[...], TILE_PIX)

    def look_up(t, found):
        for u in range(ROWS):
            n = t * ROWS + u
            found = jnp.where(tile == n, tile_slot[n], found)
        return found

    slot = lax.fori_loop(0, tile_slot.shape[0] // ROWS, look_up, jnp.zeros_like(tile))
    owner, place = split_by(slot, tiles_dev)
    half, low = split_by(within, LANES)
    owner_v[...] = jnp.full(owner_v.shape, -1, jnp.int32)
    owner_v[pl.ds(ROWS, steps), :] = owner
    pixel_v[0:steps, :] = half * tiles_dev + place
    pixel_v[steps : 2 * steps, :] = low

    a = lax.broadcasted_iota(jnp.int32, (LANES, LANES), 0)
    b = lax.broadcasted_iota(jnp.int32, (LANES, LANES), 1)
    tri[...] = jnp.where(a < b, 1.0, 0.0).astype(jnp.bfloat16)
    a = lax.broadcasted_iota(jnp.int32, spread.shape, 0)
    b = lax.broadcasted_iota(jnp.int32, spread.shape, 1)
    spread[...] = jnp.where(a % ROWS == b // LANES, 1.0, 0.0).astype(jnp.bfloat16)
    packed[...] = jnp.zeros_like(packed)
    acc_b[...] = jnp.zeros_like(acc_b)

    for fill in fills:
        fill.wait()
    flat = table.reshape((cx + 2) * pitch_y * ROWS, LANES)
    cells = table.reshape((cx + 2) * pitch_y, ROWS, LANES)
    for x in range(cx):
        hide(flat, ((x + 1) * pitch_y + 1) * ROWS, count_row[:, x : x + 1])
    to_scalar.wait()
    for halo in halos:
        halo.wait()

    own_iota = lax.broadcasted_iota(jnp.int32, (owners, LANES), 0)
    cap_iota = lax.broadcasted_iota(jnp.int32, (cap_rows * LANES, LANES), 0).astype(jnp.float32)

    def widen(step, wide):
        value = points_v[:, pl.ds(pl.multiple_of(step * LANES, LANES), LANES)]
        pieces = []
        for _ in range(3):
            high = value.astype(jnp.bfloat16)
            pieces.append(high)
            value = value - high.astype(jnp.float32)
        wide[...] = lax.dot_general(
            jnp.concatenate(pieces, axis=0), spread[...], (((0,), (0,)), ((), ())),
            preferred_element_type=jnp.float32,
        )

    def load_group(step, g, stage):
        for p in range(ROWS):
            cell = base_s[step, g * ROWS + p]
            for k, (dx, dy) in enumerate(SQUARE):
                stage[pl.ds(g * GROUP + k * ROWS * PITCH + p, ROWS, stride=PITCH), :] = cells[
                    cell + (dx * pitch_y + dy)
                ]

    def sum_group(g, stage, wide, acc):
        here = slice(g * ROWS, g * ROWS + ROWS)
        x0, y0, z0 = (wide[here, n * LANES : (n + 1) * LANES] for n in range(3))
        xs, ys = (x0, x0 - 1.0), (y0, y0 - 1.0)
        totals = [None] * 3
        for k, (dx, dy) in enumerate(SQUARE):
            def chan(c):
                return stage[pl.ds(g * GROUP + (k * ROWS + c) * PITCH, ROWS), :]

            ex, ey, ez = chan(0) - xs[dx], chan(1) - ys[dy], chan(2) - z0
            d2 = ex * ex + ey * ey + ez * ez
            w = jnp.maximum(1.0 - d2 * INV_RADIUS_SQ, 0.0)
            for c in range(3):
                term = w * chan(3 + c)
                totals[c] = term if k == 0 else totals[c] + term
        for c in range(3):
            acc[c, here, :] = totals[c]

    def pack(step, row, acc, carry):
        span = pl.ds(pl.multiple_of(step * LANES, LANES), LANES)
        mine = own_iota == owner_v[pl.ds(row, 1), :]
        hot = jnp.where(mine, 1.0, 0.0)
        before = jnp.dot(hot.astype(jnp.bfloat16), tri[...], preferred_element_type=jnp.float32)
        rank = jnp.sum(jnp.where(mine, before + carry, 0.0), axis=0, keepdims=True)
        values = []
        for c in range(3):
            rad = jnp.sum(acc[c].T, axis=0, keepdims=True) * albedo[c : c + 1, span]
            high = rad.astype(jnp.bfloat16).astype(jnp.float32)
            values += [high, rad - high]
        for n in range(2):
            values.append(pixel_v[pl.ds(n * steps + step, 1), :].astype(jnp.float32))
        left = jnp.concatenate(
            [jnp.where(mine, v, 0.0).astype(jnp.bfloat16) for v in values], axis=0
        )
        right = jnp.where(cap_iota == rank, 1.0, 0.0).astype(jnp.bfloat16)
        return left, right, carry + jnp.sum(hot, axis=1, keepdims=True)

    def half_step(now, later, was, row, stages, wides, accs, carry):
        result = pack(was, row, accs[1], carry)
        widen(later, wides[1])
        for g in range(LANES // ROWS):
            load_group(later, g, stages[1])
            sum_group(g, stages[0], wides[0], accs[0])
        return result

    def two_steps(i, carry):
        n = 2 * i
        left_a, right_a, carry = half_step(
            n, n + 1, jnp.maximum(n - 1, 0), n + ROWS - 1,
            (stage_a, stage_b), (wide_a, wide_b), (acc_a, acc_b), carry,
        )
        left_b, right_b, carry = half_step(
            n + 1, jnp.minimum(n + 2, steps - 1), n, n + ROWS,
            (stage_b, stage_a), (wide_b, wide_a), (acc_b, acc_a), carry,
        )
        packed[...] += lax.dot_general(
            jnp.concatenate([left_a, left_b], axis=1), jnp.concatenate([right_a, right_b], axis=1),
            NT, preferred_element_type=jnp.float32,
        )
        return carry

    widen(0, wide_a)
    for g in range(LANES // ROWS):
        load_group(0, g, stage_a)
    carry = lax.fori_loop(0, steps // 2, two_steps, jnp.zeros((owners, 1), jnp.float32))
    last, right_side, _ = pack(steps - 1, steps + ROWS - 1, acc_b, carry)
    packed[...] += lax.dot_general(last, right_side, NT, preferred_element_type=jnp.float32)

    flat_send = send.reshape(owners * pitch, LANES)

    def part(v, j):
        return packed[pl.ds(v * owners, owners), pl.ds(j * LANES, LANES)]

    for j in range(cap_rows):
        for c in range(3):
            flat_send[pl.ds(c * cap_rows + j, owners, stride=pitch), :] = (
                part(2 * c, j) + part(2 * c + 1, j)
            )
        flat_send[pl.ds(3 * cap_rows + j, owners, stride=pitch), :] = (
            part(6, j) * float(LANES) + part(7, j)
        )

    def copy_to(s):
        to = lax.rem(me + s, owners)
        return pltpu.make_async_remote_copy(
            src_ref=send.at[to, pl.ds(0, used)],
            dst_ref=recv.at[me, pl.ds(0, used)],
            send_sem=send_sem.at[to],
            recv_sem=recv_sem.at[me],
            device_id=(to // ny, lax.rem(to, ny)),
            device_id_type=MESH,
        )

    def go(s, _):
        copy_to(s).start()
        return 0

    lax.fori_loop(1, owners, go, 0)
    recv[me] = send[me]

    halves = out.shape[2] // LANES
    high_rows = tiles_dev * halves
    high_iota = lax.broadcasted_iota(jnp.int32, (high_rows, LANES), 0).astype(jnp.float32)
    low_iota = lax.broadcasted_iota(jnp.int32, (LANES, LANES), 0).astype(jnp.float32)

    def arrive(s):
        come = lax.rem(me + owners - s, owners)

        @pl.when(s > 0)
        def _():
            pltpu.make_async_remote_copy(
                src_ref=send.at[come, pl.ds(0, used)],
                dst_ref=recv.at[come, pl.ds(0, used)],
                send_sem=send_sem.at[come],
                recv_sem=recv_sem.at[come],
                device_id=(come // ny, lax.rem(come, ny)),
                device_id_type=MESH,
            ).wait_recv()

        return come

    def add(step, total):
        lefts, rights = [], []
        sources = [arrive(step * 4 + u) for u in range(4)]
        for come in sources:
            blk = recv[come]
            for j in range(cap_rows):
                def row(v):
                    r = v * cap_rows + j
                    return blk[r : r + 1]

                where = row(3)
                high = jnp.floor(where * (1.0 / LANES))
                here = high_iota == high
                pieces = []
                for c in range(3):
                    value = row(c)
                    top = value.astype(jnp.bfloat16).astype(jnp.float32)
                    pieces += [jnp.where(here, top, 0.0), jnp.where(here, value - top, 0.0)]
                lefts.append(jnp.concatenate(pieces, axis=0).astype(jnp.bfloat16))
                rights.append(
                    jnp.where(low_iota == where - high * float(LANES), 1.0, 0.0).astype(jnp.bfloat16)
                )
        left = jnp.concatenate(lefts, axis=1)
        right = jnp.concatenate(rights, axis=1)
        return total + lax.dot_general(left, right, NT, preferred_element_type=jnp.float32)

    total = lax.fori_loop(0, owners // 4, add, jnp.zeros((6 * high_rows, LANES), jnp.float32))
    for c in range(3):
        for h in range(halves):
            at = 2 * c * high_rows + h * tiles_dev
            out[c, :, h * LANES : (h + 1) * LANES] = (
                total[at : at + tiles_dev] + total[at + high_rows : at + high_rows + tiles_dev]
            )

    def sent(s, _):
        copy_to(s).wait_send()
        return 0

    lax.fori_loop(1, owners, sent, 0)


def per_device(
    nx, ny, photon_data, block_counts, gather_offsets, gather_blocks, albedo, gather_pixels, tile_slot
):
    cx, cy = photon_data.shape[1:3]
    points = gather_offsets.shape[1]
    steps = points // LANES
    owners = nx * ny
    tiles = tile_slot.shape[0]
    tiles_dev = tiles // owners
    cap_rows = -(-(3 * points // owners) // LANES)
    pitch = -(-4 * cap_rows // ROWS) * ROWS
    vm = pl.BlockSpec(memory_space=pltpu.VMEM)
    smem = pl.BlockSpec(memory_space=pltpu.SMEM)
    dma, f32 = pltpu.SemaphoreType.DMA, jnp.float32
    table_rows = LANES // ROWS * GROUP
    return pl.pallas_call(
        functools.partial(whole_kernel, nx, ny, cap_rows, tiles_dev),
        out_shape=jax.ShapeDtypeStruct((3, tiles_dev, TILE_PIX), f32),
        in_specs=[pl.BlockSpec(memory_space=pl.ANY)] + [vm] * 5 + [smem],
        out_specs=vm,
        scratch_shapes=[
            pltpu.VMEM((cx + 2, cy + 2, ROWS, LANES), f32),
            pltpu.VMEM((2, cy, ROWS, LANES), f32),
            pltpu.VMEM((2, cx, ROWS, LANES), f32),
            pltpu.VMEM((table_rows, LANES), f32),
            pltpu.VMEM((table_rows, LANES), f32),
            pltpu.VMEM((LANES, 3 * LANES), f32),
            pltpu.VMEM((LANES, 3 * LANES), f32),
            pltpu.VMEM((3, LANES, LANES), f32),
            pltpu.VMEM((3, LANES, LANES), f32),
            pltpu.VMEM((3 * ROWS, 3 * LANES), jnp.bfloat16),
            pltpu.VMEM((LANES, LANES), jnp.bfloat16),
            pltpu.VMEM((cy, cx), f32),
            pltpu.VMEM((LANES, LANES), f32),
            pltpu.VMEM((ROWS, points), f32),
            pltpu.VMEM((steps, LANES), jnp.int32),
            pltpu.SMEM((steps, LANES), jnp.int32),
            pltpu.VMEM((steps + ROWS, LANES), jnp.int32),
            pltpu.VMEM((2 * steps, LANES), jnp.int32),
            pltpu.VMEM((8 * owners, cap_rows * LANES), f32),
            pltpu.VMEM((owners, pitch, LANES), f32),
            pltpu.VMEM((owners, pitch, LANES), f32),
            dma((CHANNELS,)),
            dma((4 * CHANNELS,)),
            dma,
            dma((8,)),
            dma((8,)),
            dma((owners,)),
            dma((owners,)),
        ],
        compiler_params=pltpu.CompilerParams(collective_id=0, has_side_effects=True),
        name="estimate",
    )(
        photon_data, block_counts.T, gather_offsets, gather_blocks, albedo,
        gather_pixels.reshape(steps, LANES), tile_slot,
    )


def solution(mesh):
    both = ("bx", "by")
    in_specs = (
        P(None, "bx", "by", None), P("bx", "by"), P(None, both), P(None, both),
        P(None, both), P(both), P(),
    )
    return jax.shard_map(
        functools.partial(per_device, mesh.shape["bx"], mesh.shape["by"]),
        mesh=mesh, in_specs=in_specs, out_specs=P(None, both, None), check_vma=False,
    )
```

time: 83.6 us -> 45.4 us (0.54)
  Pallas kernels: 70.3 us -> 43.8 us
  other arithmetic: 8.78 us -> 0 us
  local copies, waits for them, and re-layouts: 3.87 us -> 1.35 us
    pallas_call x3 -> x1, Pallas kernels: 70.3 us -> 43.8 us  [per_device(): pl.pallas_call(functools.partial(whole_kernel, nx, ny, cap_rows, tiles_de...]
    select_n x3 -> x0, other arithmetic: 3.34 us -> none  [the longest x1 2.54 us: per_device(): first = jnp.where(live, photon_data[0], FAR)]
    reduce_sum x1 -> x0, other arithmetic: 1.96 us -> none  [per_device(): slot = jnp.sum(jnp.where(matched, tile_slot[None, :], 0), axis=1)]
    unnamed x3 -> x1, local copies, waits for them, and re-layouts: 2.77 us -> 1.35 us
    unnamed x1 -> x0, other arithmetic: 1.2 us -> none
    slice x3 -> x0, local copies, waits for them, and re-layouts: 1.02 us -> none  [the longest x1 1 us: per_device(): gather_offsets[0:1] - shift_x]
where the time goes in v1:
time: 45.4 us; the launch traced here: 45.2 us
  Pallas kernels  43.8 us (96%)
  local copies, waits for them, and re-layouts  1.35 us (3%)
    pallas_call x1, Pallas kernels, per_device(): pl.pallas_call(functools.partial(whole_kernel, nx, ny, cap_rows, tiles_de...  43.8 us
    unnamed x1, local copies, waits for them, and re-layouts  1.35 us

profile of v1, /device:TPU:0, one launch (start us, length us, event | category | flops | bytes accessed | tf_op | source)
XLA Modules:
  0.0 45.2 jit_solution(12887173734272306852)
XLA Ops:
  0.0 43.8 %estimate.1 = f32[3,8,256]{2,1,0:T(8,128)} custom-call(f32[6,64,32,128]{3,2,1,0:T(8,128)} %photons.1, s32[32,64]{1,0:T(8,128)} %bitcast.2, f32[3,4096]{1,0:T(4,128)} %offsets.1, s32[4,4096]{1,0:T(4,128)} %blocks.1, f32[3,4096]{1,0:T(4,128)} %albedo.1, s32[32,128]{1,0:T(8,128)} %bitcast.3, s32[256]{0:T(256)} %tile_slot.1), custom_call_target="tpu_custom_call" | custom-call | tf_op jit(solution)/shard_map/estimate/pallas_call | solution.py:385
  43.9 1.3 %copy.9 = f32[3,8,256]{2,1,0:T(8,128)} copy(f32[3,8,256]{2,1,0:T(8,128)} %estimate.1) | data formatting | bytes 49152

commit v2 on v1

v2 whole, which is shorter than its diff:
```python
import functools

import jax
import jax.numpy as jnp
from jax import lax
from jax.experimental import pallas as pl
from jax.experimental.pallas import tpu as pltpu
from jax.sharding import PartitionSpec as P

TILE_PIX = 256
INV_RADIUS_SQ = 4.0
FAR = 1.0e4
LANES = 128
ROWS = 8
CHANNELS = 6
MESH = pl.DeviceIdType.MESH
NT = (((1,), (1,)), ((), ()))
PITCH = 9
GROUP = 2 * ROWS * PITCH


def split_by(value, size):
    if size & (size - 1) == 0:
        return value >> (size.bit_length() - 1), value & (size - 1)
    return lax.div(value, size), lax.rem(value, size)


def whole_kernel(
    nx, ny, cap_rows, tiles_dev,
    photons, counts_h, offsets_h, blocks_h, albedo_h, pixels_h, tile_slot_h, out,
    table, edge_x, edge_y, ring_y, stage_a, stage_b, wide_a, wide_b, acc_a, acc_b, partial,
    spread, tri, counts, offsets, blocks, albedo, pixels, tile_slot,
    count_row, count_col, points_v, base_v, base_s, owner_v, left_v, right_v,
    packed, packed_at, send, recv,
    fill_sem, edge_sem, small_sem, base_sem, halo_send, halo_recv, send_sem, recv_sem,
):
    cx, cy = photons.shape[1], photons.shape[2]
    pitch_y = cy + 2
    grid_x, grid_y = cx * nx, cy * ny
    points = offsets.shape[1]
    steps = points // LANES
    owners = nx * ny
    pitch = send.shape[1]
    used = 4 * cap_rows
    ix, iy = lax.axis_index("bx"), lax.axis_index("by")
    me = ix * ny + iy

    barrier = pltpu.get_barrier_semaphore()

    def greet(s, _):
        to = lax.rem(me + s, owners)
        pl.semaphore_signal(
            barrier, inc=1, device_id=(to // ny, lax.rem(to, ny)), device_id_type=MESH
        )
        return 0

    lax.fori_loop(1, owners, greet, 0)

    small = [
        pltpu.make_async_copy(src, dst, small_sem.at[n])
        for n, (src, dst) in enumerate(
            (
                (counts_h, counts), (blocks_h, blocks), (offsets_h, offsets),
                (pixels_h, pixels), (tile_slot_h, tile_slot), (albedo_h, albedo),
            )
        )
    ]
    edges = []
    for c in range(CHANNELS):
        for s, x in enumerate((cx - 1, 0)):
            edges.append(
                pltpu.make_async_copy(
                    photons.at[c, x], edge_x.at[s, :, c], edge_sem.at[len(edges)]
                )
            )
        for s, y in enumerate((cy - 1, 0)):
            edges.append(
                pltpu.make_async_copy(
                    photons.at[c, :, y], edge_y.at[s, :, c], edge_sem.at[len(edges)]
                )
            )
    fills = [
        pltpu.make_async_copy(
            photons.at[c], table.at[pl.ds(1, cx), pl.ds(1, cy), c], fill_sem.at[c]
        )
        for c in range(CHANNELS)
    ]
    small[0].start()
    for edge in edges:
        edge.start()
    for copy in small[1:]:
        copy.start()
    for fill in fills:
        fill.start()

    small[0].wait()
    count_row[...] = counts[...].astype(jnp.float32)
    square = jnp.concatenate(
        [count_row[...], jnp.zeros((cy, LANES - cx), jnp.float32)], axis=1
    )
    square = jnp.concatenate([square, jnp.zeros((LANES - cy, LANES), jnp.float32)], axis=0)
    count_col[...] = square.T
    lane = lax.broadcasted_iota(jnp.int32, (ROWS, LANES), 1).astype(jnp.float32)

    def hide(ref, first, column):
        rows = column.shape[0]
        for r in range(0, rows, ROWS):
            place = pl.ds(first + r * ROWS, ROWS, stride=ROWS)
            ref[place, :] = jnp.where(lane < column[r : r + ROWS], ref[place, :], FAR)

    for edge in edges:
        edge.wait()
    flat_x = edge_x.reshape(2 * cy * ROWS, LANES)
    flat_y = edge_y.reshape(2 * cx * ROWS, LANES)
    for s, y in enumerate((cy - 1, 0)):
        hide(flat_y, s * cx * ROWS, count_col[0:cx, y : y + 1])
    for s, x in enumerate((cx - 1, 0)):
        hide(flat_x, s * cy * ROWS, count_row[:, x : x + 1])
    pl.semaphore_wait(barrier, owners - 1)

    right, left = lax.rem(ix + 1, nx), lax.rem(ix + nx - 1, nx)
    up, down = lax.rem(iy + 1, ny), lax.rem(iy + ny - 1, ny)
    data = pl.ds(0, CHANNELS)
    wide_x, wide_y = pl.ds(1, cx), pl.ds(1, cy)
    parts = [
        (edge_y.at[0, :, data], ring_y.at[0, wide_x, data], ix, up),
        (edge_y.at[1, :, data], ring_y.at[1, wide_x, data], ix, down),
        (edge_x.at[0, :, data], table.at[0, wide_y, data], right, iy),
        (edge_x.at[1, :, data], table.at[cx + 1, wide_y, data], left, iy),
        (edge_x.at[0, cy - 1, data], ring_y.at[0, 0, data], right, up),
        (edge_x.at[0, 0, data], ring_y.at[1, 0, data], right, down),
        (edge_x.at[1, cy - 1, data], ring_y.at[0, cx + 1, data], left, up),
        (edge_x.at[1, 0, data], ring_y.at[1, cx + 1, data], left, down),
    ]
    halos = [
        pltpu.make_async_remote_copy(
            src_ref=src, dst_ref=dst, send_sem=halo_send.at[n], recv_sem=halo_recv.at[n],
            device_id=(px, py), device_id_type=MESH,
        )
        for n, (src, dst, px, py) in enumerate(parts)
    ]
    for halo in halos:
        halo.start()

    for copy in small[1:4]:
        copy.wait()
    cell_x, cell_y = split_by(blocks[...], grid_y)

    def local(cell, first, size):
        t = cell - first + 1
        t = jnp.where(t < 0, t + size, t)
        return jnp.where(t >= size, t - size, t)

    lx, ly = local(cell_x, ix * cx, grid_x), local(cell_y, iy * cy, grid_y)
    low_x, low_y = jnp.min(lx, axis=0, keepdims=True), jnp.min(ly, axis=0, keepdims=True)
    own_y = ly[0:1]
    other_y = 2 * low_y + 1 - own_y
    line = jnp.minimum(low_x, cx) * pitch_y
    bases = (
        line + jnp.clip(own_y, 0, cy + 1),
        line + jnp.clip(other_y, 0, cy + 1),
    )
    for n in range(2):
        for j in range(steps):
            base_v[n * steps + j : n * steps + j + 1, :] = bases[n][:, j * LANES : (j + 1) * LANES]
    to_scalar = pltpu.make_async_copy(base_v, base_s, base_sem)
    to_scalar.start()
    points_v[...] = jnp.zeros_like(points_v)
    points_v[0:1, :] = offsets[0:1, :] + (lx[0:1] - low_x).astype(jnp.float32)
    points_v[1:2, :] = offsets[1:2, :]
    points_v[2:3, :] = offsets[2:3, :]
    points_v[3:4, :] = offsets[1:2, :] + (own_y - other_y).astype(jnp.float32)

    tile, within = split_by(pixels[...], TILE_PIX)
    small[4].wait()

    def look_up(t, found):
        for u in range(ROWS):
            n = t * ROWS + u
            found = jnp.where(tile == n, tile_slot[n], found)
        return found

    slot = lax.fori_loop(0, tile_slot.shape[0] // ROWS, look_up, jnp.zeros_like(tile))
    owner, place = split_by(slot, tiles_dev)
    half, low = split_by(within, LANES)
    first = half * tiles_dev + place
    owner_v[...] = jnp.full(owner_v.shape, -1, jnp.int32)
    owner_v[pl.ds(ROWS, steps), :] = owner

    a = lax.broadcasted_iota(jnp.int32, (LANES, LANES), 0)
    b = lax.broadcasted_iota(jnp.int32, (LANES, LANES), 1)
    tri[...] = jnp.where(a < b, 1.0, 0.0).astype(jnp.bfloat16)
    for n, rows in enumerate(((0, 1, 2), (0, 3, 2))):
        a = lax.broadcasted_iota(jnp.int32, spread.shape[1:], 0) % ROWS
        b = lax.broadcasted_iota(jnp.int32, spread.shape[1:], 1) // LANES
        hit = (a == rows[0]) & (b == 0)
        for m in range(1, 3):
            hit = hit | ((a == rows[m]) & (b == m))
        spread[n] = jnp.where(hit, 1.0, 0.0).astype(jnp.bfloat16)
    packed[...] = jnp.zeros_like(packed)
    acc_b[...] = jnp.zeros_like(acc_b)

    own_iota = lax.broadcasted_iota(jnp.int32, (owners, LANES), 0)
    cap_iota = lax.broadcasted_iota(jnp.int32, (cap_rows * LANES, LANES), 0).astype(jnp.float32)
    nothing = jnp.zeros((2 * owners, LANES), jnp.bfloat16)
    empty = jnp.zeros((cap_rows * LANES, LANES), jnp.bfloat16)
    for at in (0, steps + 1):
        left_v[:, at * LANES : (at + 1) * LANES] = nothing
        right_v[:, at * LANES : (at + 1) * LANES] = empty
    carry = jnp.zeros((owners, LANES), jnp.float32)
    ones = jnp.ones((LANES, LANES), jnp.bfloat16)
    for j in range(steps):
        mine = own_iota == owner[j : j + 1, :]
        hot = jnp.where(mine, 1.0, 0.0).astype(jnp.bfloat16)
        before = jnp.dot(hot, tri[...], preferred_element_type=jnp.float32)
        rank = jnp.sum(jnp.where(mine, before + carry, 0.0), axis=0, keepdims=True)
        carry = carry + jnp.dot(hot, ones, preferred_element_type=jnp.float32)
        span = slice((j + 1) * LANES, (j + 2) * LANES)
        left_v[:, span] = jnp.concatenate(
            [
                jnp.where(mine, v[j : j + 1, :].astype(jnp.float32), 0.0).astype(jnp.bfloat16)
                for v in (first, low)
            ],
            axis=0,
        )
        right_v[:, span] = jnp.where(cap_iota == rank, 1.0, 0.0).astype(jnp.bfloat16)
    packed_at[...] = lax.dot_general(
        left_v[...], right_v[...], NT, preferred_element_type=jnp.float32
    )

    for fill in fills:
        fill.wait()
    flat = table.reshape((cx + 2) * pitch_y * ROWS, LANES)
    cells = table.reshape((cx + 2) * pitch_y, ROWS, LANES)
    for x in range(cx):
        hide(flat, ((x + 1) * pitch_y + 1) * ROWS, count_row[:, x : x + 1])
    small[5].wait()
    to_scalar.wait()

    def widen(n, step, wide):
        value = points_v[:, pl.ds(pl.multiple_of(step * LANES, LANES), LANES)]
        pieces = []
        for _ in range(3):
            high = value.astype(jnp.bfloat16)
            pieces.append(high)
            value = value - high.astype(jnp.float32)
        wide[...] = lax.dot_general(
            jnp.concatenate(pieces, axis=0), spread[n], (((0,), (0,)), ((), ())),
            preferred_element_type=jnp.float32,
        )

    def load_group(n, step, g, stage):
        for p in range(ROWS):
            cell = base_s[n * steps + step, g * ROWS + p]
            for k in range(2):
                stage[pl.ds(g * GROUP + k * ROWS * PITCH + p, ROWS, stride=PITCH), :] = cells[
                    cell + k * pitch_y
                ]

    def sum_group(g, stage, wide, totals):
        here = slice(g * ROWS, g * ROWS + ROWS)
        x0, y0, z0 = (wide[here, n * LANES : (n + 1) * LANES] for n in range(3))
        for k, x in enumerate((x0, x0 - 1.0)):
            def chan(c):
                return stage[pl.ds(g * GROUP + (k * ROWS + c) * PITCH, ROWS), :]

            ex, ey, ez = chan(0) - x, chan(1) - y0, chan(2) - z0
            d2 = ex * ex + ey * ey + ez * ez
            w = jnp.maximum(1.0 - d2 * INV_RADIUS_SQ, 0.0)
            for c in range(3):
                term = w * chan(3 + c)
                totals[c] = term if totals[c] is None else totals[c] + term
        return totals

    def first_half(now, later, stages, wides):
        widen(0, later, wides[1])
        for g in range(LANES // ROWS):
            load_group(0, later, g, stages[1])
            totals = sum_group(g, stages[0], wides[0], [None] * 3)
            for c in range(3):
                partial[now, c, g * ROWS : (g + 1) * ROWS, :] = totals[c]

    def first_two(i, _):
        n = 2 * i
        first_half(n, n + 1, (stage_a, stage_b), (wide_a, wide_b))
        first_half(n + 1, jnp.minimum(n + 2, steps - 1), (stage_b, stage_a), (wide_b, wide_a))
        return 0

    for halo in halos[2:4]:
        halo.wait()
    widen(0, 0, wide_a)
    for g in range(LANES // ROWS):
        load_group(0, 0, g, stage_a)
    lax.fori_loop(0, steps // 2, first_two, 0)

    for halo in halos[:2] + halos[4:]:
        halo.wait()
    for s, y in enumerate((0, cy + 1)):
        for x in range(cx + 2):
            table[x, y] = ring_y[s, x]

    def radiance(step, acc):
        span = pl.ds(pl.multiple_of(step * LANES, LANES), LANES)
        return [
            jnp.sum(acc[c].T, axis=0, keepdims=True) * albedo[c : c + 1, span] for c in range(3)
        ]

    def pack(row, values):
        mine = own_iota == owner_v[pl.ds(row, 1), :]
        pieces = []
        for rad in values:
            high = rad.astype(jnp.bfloat16).astype(jnp.float32)
            pieces += [high, rad - high]
        return jnp.concatenate(
            [jnp.where(mine, v, 0.0).astype(jnp.bfloat16) for v in pieces], axis=0
        )

    def second_half(now, later, was, row, stages, wides, accs):
        side = pack(row, radiance(was, accs[1]))
        widen(1, later, wides[1])
        for g in range(LANES // ROWS):
            load_group(1, later, g, stages[1])
            here = slice(g * ROWS, (g + 1) * ROWS)
            totals = sum_group(g, stages[0], wides[0], [partial[now, c, here, :] for c in range(3)])
            for c in range(3):
                accs[0][c, here, :] = totals[c]
        return side

    def add_packed(sides, pair, width):
        span = pl.ds(pl.multiple_of(pair * 2 * LANES, LANES), width)
        packed[...] += lax.dot_general(
            jnp.concatenate(sides, axis=1), right_v[:, span], NT, preferred_element_type=jnp.float32
        )

    def second_two(i, _):
        n = 2 * i
        side_a = second_half(
            n, n + 1, jnp.maximum(n - 1, 0), n + ROWS - 1,
            (stage_a, stage_b), (wide_a, wide_b), (acc_a, acc_b),
        )
        side_b = second_half(
            n + 1, jnp.minimum(n + 2, steps - 1), n, n + ROWS,
            (stage_b, stage_a), (wide_b, wide_a), (acc_b, acc_a),
        )
        add_packed([side_a, side_b], i, 2 * LANES)
        return 0

    widen(1, 0, wide_a)
    for g in range(LANES // ROWS):
        load_group(1, 0, g, stage_a)
    lax.fori_loop(0, steps // 2, second_two, 0)
    add_packed([pack(steps + ROWS - 1, radiance(steps - 1, acc_b))], steps // 2, LANES)

    flat_send = send.reshape(owners * pitch, LANES)

    def part(v, j):
        return packed[pl.ds(v * owners, owners), pl.ds(j * LANES, LANES)]

    for j in range(cap_rows):
        for c in range(3):
            flat_send[pl.ds(c * cap_rows + j, owners, stride=pitch), :] = (
                part(2 * c, j) + part(2 * c + 1, j)
            )
        flat_send[pl.ds(3 * cap_rows + j, owners, stride=pitch), :] = (
            packed_at[0:owners, j * LANES : (j + 1) * LANES] * float(LANES)
            + packed_at[owners : 2 * owners, j * LANES : (j + 1) * LANES]
        )

    def copy_to(s):
        to = lax.rem(me + s, owners)
        return pltpu.make_async_remote_copy(
            src_ref=send.at[to, pl.ds(0, used)],
            dst_ref=recv.at[me, pl.ds(0, used)],
            send_sem=send_sem.at[to],
            recv_sem=recv_sem.at[me],
            device_id=(to // ny, lax.rem(to, ny)),
            device_id_type=MESH,
        )

    def go(s, _):
        copy_to(s).start()
        return 0

    lax.fori_loop(1, owners, go, 0)
    recv[me] = send[me]

    halves = out.shape[2] // LANES
    high_rows = tiles_dev * halves
    high_iota = lax.broadcasted_iota(jnp.int32, (high_rows, LANES), 0).astype(jnp.float32)
    low_iota = lax.broadcasted_iota(jnp.int32, (LANES, LANES), 0).astype(jnp.float32)

    def arrive(s):
        come = lax.rem(me + owners - s, owners)

        @pl.when(s > 0)
        def _():
            pltpu.make_async_remote_copy(
                src_ref=send.at[come, pl.ds(0, used)],
                dst_ref=recv.at[come, pl.ds(0, used)],
                send_sem=send_sem.at[come],
                recv_sem=recv_sem.at[come],
                device_id=(come // ny, lax.rem(come, ny)),
                device_id_type=MESH,
            ).wait_recv()

        return come

    def add(step, total):
        lefts, rights = [], []
        sources = [arrive(step * 4 + u) for u in range(4)]
        for come in sources:
            blk = recv[come]
            for j in range(cap_rows):
                def row(v):
                    r = v * cap_rows + j
                    return blk[r : r + 1]

                where = row(3)
                high = jnp.floor(where * (1.0 / LANES))
                here = high_iota == high
                pieces = []
                for c in range(3):
                    value = row(c)
                    top = value.astype(jnp.bfloat16).astype(jnp.float32)
                    pieces += [jnp.where(here, top, 0.0), jnp.where(here, value - top, 0.0)]
                lefts.append(jnp.concatenate(pieces, axis=0).astype(jnp.bfloat16))
                rights.append(
                    jnp.where(low_iota == where - high * float(LANES), 1.0, 0.0).astype(jnp.bfloat16)
                )
        left = jnp.concatenate(lefts, axis=1)
        right = jnp.concatenate(rights, axis=1)
        return total + lax.dot_general(left, right, NT, preferred_element_type=jnp.float32)

    total = lax.fori_loop(0, owners // 4, add, jnp.zeros((6 * high_rows, LANES), jnp.float32))
    for c in range(3):
        for h in range(halves):
            at = 2 * c * high_rows + h * tiles_dev
            out[c, :, h * LANES : (h + 1) * LANES] = (
                total[at : at + tiles_dev] + total[at + high_rows : at + high_rows + tiles_dev]
            )

    def sent(s, _):
        copy_to(s).wait_send()
        return 0

    lax.fori_loop(1, owners, sent, 0)


def per_device(
    nx, ny, photon_data, block_counts, gather_offsets, gather_blocks, albedo, gather_pixels, tile_slot
):
    cx, cy = photon_data.shape[1:3]
    points = gather_offsets.shape[1]
    steps = points // LANES
    owners = nx * ny
    tiles = tile_slot.shape[0]
    tiles_dev = tiles // owners
    cap_rows = -(-(3 * points // owners) // LANES)
    pitch = -(-4 * cap_rows // ROWS) * ROWS
    hb, vm = pl.BlockSpec(memory_space=pl.ANY), pl.BlockSpec(memory_space=pltpu.VMEM)
    dma, f32, i32, bf16 = pltpu.SemaphoreType.DMA, jnp.float32, jnp.int32, jnp.bfloat16
    stage_rows = LANES // ROWS * GROUP
    return pl.pallas_call(
        functools.partial(whole_kernel, nx, ny, cap_rows, tiles_dev),
        out_shape=jax.ShapeDtypeStruct((3, tiles_dev, TILE_PIX), f32),
        in_specs=[hb] * 7,
        out_specs=vm,
        scratch_shapes=[
            pltpu.VMEM((cx + 2, cy + 2, ROWS, LANES), f32),
            pltpu.VMEM((2, cy, ROWS, LANES), f32),
            pltpu.VMEM((2, cx, ROWS, LANES), f32),
            pltpu.VMEM((2, cx + 2, ROWS, LANES), f32),
            pltpu.VMEM((stage_rows, LANES), f32),
            pltpu.VMEM((stage_rows, LANES), f32),
            pltpu.VMEM((LANES, 3 * LANES), f32),
            pltpu.VMEM((LANES, 3 * LANES), f32),
            pltpu.VMEM((3, LANES, LANES), f32),
            pltpu.VMEM((3, LANES, LANES), f32),
            pltpu.VMEM((steps, 3, LANES, LANES), f32),
            pltpu.VMEM((2, 3 * ROWS, 3 * LANES), bf16),
            pltpu.VMEM((LANES, LANES), bf16),
            pltpu.VMEM((cy, cx), i32),
            pltpu.VMEM((3, points), f32),
            pltpu.VMEM((4, points), i32),
            pltpu.VMEM((3, points), f32),
            pltpu.VMEM((steps, LANES), i32),
            pltpu.SMEM((tiles,), i32),
            pltpu.VMEM((cy, cx), f32),
            pltpu.VMEM((LANES, LANES), f32),
            pltpu.VMEM((ROWS, points), f32),
            pltpu.VMEM((2 * steps, LANES), i32),
            pltpu.SMEM((2 * steps, LANES), i32),
            pltpu.VMEM((steps + ROWS, LANES), i32),
            pltpu.VMEM((2 * owners, points + 2 * LANES), bf16),
            pltpu.VMEM((cap_rows * LANES, points + 2 * LANES), bf16),
            pltpu.VMEM((6 * owners, cap_rows * LANES), f32),
            pltpu.VMEM((2 * owners, cap_rows * LANES), f32),
            pltpu.VMEM((owners, pitch, LANES), f32),
            pltpu.VMEM((owners, pitch, LANES), f32),
            dma((CHANNELS,)),
            dma((4 * CHANNELS,)),
            dma((6,)),
            dma,
            dma((8,)),
            dma((8,)),
            dma((owners,)),
            dma((owners,)),
        ],
        compiler_params=pltpu.CompilerParams(collective_id=0, has_side_effects=True),
        name="estimate",
    )(
        photon_data, block_counts.T, gather_offsets, gather_blocks, albedo,
        gather_pixels.reshape(steps, LANES), tile_slot,
    )


def solution(mesh):
    both = ("bx", "by")
    in_specs = (
        P(None, "bx", "by", None), P("bx", "by"), P(None, both), P(None, both),
        P(None, both), P(both), P(),
    )
    return jax.shard_map(
        functools.partial(per_device, mesh.shape["bx"], mesh.shape["by"]),
        mesh=mesh, in_specs=in_specs, out_specs=P(None, both, None), check_vma=False,
    )
```

time: 45.4 us -> 38.7 us (0.85)
  Pallas kernels: 43.8 us -> 37.2 us
    pallas_call x1, Pallas kernels: 43.8 us -> 37.2 us  [per_device(): pl.pallas_call(functools.partial(whole_kernel, nx, ny, cap_rows, tiles_de...]
where the time goes in v2:
time: 38.7 us; the launch traced here: 38.5 us
  Pallas kernels  37.2 us (96%)
  local copies, waits for them, and re-layouts  1.35 us (3%)
    pallas_call x1, Pallas kernels, per_device(): pl.pallas_call(functools.partial(whole_kernel, nx, ny, cap_rows, tiles_de...  37.2 us
    unnamed x1, local copies, waits for them, and re-layouts  1.35 us

profile of v2, /device:TPU:0, one launch (start us, length us, event | category | flops | bytes accessed | tf_op | source)
XLA Modules:
  0.0 38.5 jit_solution(16601365511253585682)
XLA Ops:
  0.0 37.2 %estimate.1 = f32[3,8,256]{2,1,0:T(8,128)} custom-call(f32[6,64,32,128]{3,2,1,0:T(8,128)} %photons.1, s32[32,64]{1,0:T(8,128)} %bitcast.2, f32[3,4096]{1,0:T(4,128)} %offsets_h.1, s32[4,4096]{1,0:T(4,128)} %blocks_h.1, f32[3,4096]{1,0:T(4,128)} %albedo_h.1, s32[32,128]{1,0:T(8,128)} %bitcast.3, s32[256]{0:T(256)} %tile_slot_h.1), custom_call_target="tpu_custom_call" | custom-call | tf_op jit(solution)/shard_map/estimate/pallas_call | solution.py:463
  37.2 1.3 %copy.9 = f32[3,8,256]{2,1,0:T(8,128)} copy(f32[3,8,256]{2,1,0:T(8,128)} %estimate.1) | data formatting | bytes 49152

commit v3 on v2

--- a/solution.py
+++ b/solution.py
@@ -28,11 +28,12 @@
 def whole_kernel(
     nx, ny, cap_rows, tiles_dev,
     photons, counts_h, offsets_h, blocks_h, albedo_h, pixels_h, tile_slot_h, out,
-    table, edge_x, edge_y, ring_y, stage_a, stage_b, wide_a, wide_b, acc_a, acc_b, partial,
+    table, edge_x, edge_y, ring_y, stage_a, stage_b, wide_a, wide_b, side_v, partial,
     spread, tri, counts, offsets, blocks, albedo, pixels, tile_slot,
     count_row, count_col, points_v, base_v, base_s, owner_v, left_v, right_v,
-    packed, packed_at, send, recv,
+    packed, send, recv, send_at, recv_at,
     fill_sem, edge_sem, small_sem, base_sem, halo_send, halo_recv, send_sem, recv_sem,
+    at_send_sem, at_recv_sem,
 ):
     cx, cy = photons.shape[1], photons.shape[2]
     pitch_y = cy + 2
@@ -41,7 +42,6 @@
     steps = points // LANES
     owners = nx * ny
     pitch = send.shape[1]
-    used = 4 * cap_rows
     ix, iy = lax.axis_index("bx"), lax.axis_index("by")
     me = ix * ny + iy
 
@@ -185,7 +185,7 @@
     half, low = split_by(within, LANES)
     first = half * tiles_dev + place
     owner_v[...] = jnp.full(owner_v.shape, -1, jnp.int32)
-    owner_v[pl.ds(ROWS, steps), :] = owner
+    owner_v[2 : 2 + steps, :] = owner
 
     a = lax.broadcasted_iota(jnp.int32, (LANES, LANES), 0)
     b = lax.broadcasted_iota(jnp.int32, (LANES, LANES), 1)
@@ -198,15 +198,10 @@
             hit = hit | ((a == rows[m]) & (b == m))
         spread[n] = jnp.where(hit, 1.0, 0.0).astype(jnp.bfloat16)
     packed[...] = jnp.zeros_like(packed)
-    acc_b[...] = jnp.zeros_like(acc_b)
+    side_v[...] = jnp.zeros_like(side_v)
 
     own_iota = lax.broadcasted_iota(jnp.int32, (owners, LANES), 0)
     cap_iota = lax.broadcasted_iota(jnp.int32, (cap_rows * LANES, LANES), 0).astype(jnp.float32)
-    nothing = jnp.zeros((2 * owners, LANES), jnp.bfloat16)
-    empty = jnp.zeros((cap_rows * LANES, LANES), jnp.bfloat16)
-    for at in (0, steps + 1):
-        left_v[:, at * LANES : (at + 1) * LANES] = nothing
-        right_v[:, at * LANES : (at + 1) * LANES] = empty
     carry = jnp.zeros((owners, LANES), jnp.float32)
     ones = jnp.ones((LANES, LANES), jnp.bfloat16)
     for j in range(steps):
@@ -215,7 +210,7 @@
         before = jnp.dot(hot, tri[...], preferred_element_type=jnp.float32)
         rank = jnp.sum(jnp.where(mine, before + carry, 0.0), axis=0, keepdims=True)
         carry = carry + jnp.dot(hot, ones, preferred_element_type=jnp.float32)
-        span = slice((j + 1) * LANES, (j + 2) * LANES)
+        span = slice(j * LANES, (j + 1) * LANES)
         left_v[:, span] = jnp.concatenate(
             [
                 jnp.where(mine, v[j : j + 1, :].astype(jnp.float32), 0.0).astype(jnp.bfloat16)
@@ -224,9 +219,13 @@
             axis=0,
         )
         right_v[:, span] = jnp.where(cap_iota == rank, 1.0, 0.0).astype(jnp.bfloat16)
-    packed_at[...] = lax.dot_general(
-        left_v[...], right_v[...], NT, preferred_element_type=jnp.float32
-    )
+    packed_at = lax.dot_general(left_v[...], right_v[...], NT, preferred_element_type=jnp.float32)
+    packed_at = packed_at[:owners] * float(LANES) + packed_at[owners:]
+    flat_at = send_at.reshape(owners * send_at.shape[1], LANES)
+    for j in range(cap_rows):
+        flat_at[pl.ds(j, owners, stride=send_at.shape[1]), :] = packed_at[
+            :, j * LANES : (j + 1) * LANES
+        ]
 
     for fill in fills:
         fill.wait()
@@ -278,7 +277,7 @@
             load_group(0, later, g, stages[1])
             totals = sum_group(g, stages[0], wides[0], [None] * 3)
             for c in range(3):
-                partial[now, c, g * ROWS : (g + 1) * ROWS, :] = totals[c]
+                partial[now + 2, c, g * ROWS : (g + 1) * ROWS, :] = totals[c]
 
     def first_two(i, _):
         n = 2 * i
@@ -299,57 +298,70 @@
         for x in range(cx + 2):
             table[x, y] = ring_y[s, x]
 
-    def radiance(step, acc):
+    def copy_to(s, rows, source, target, sems):
+        to = lax.rem(me + s, owners)
+        return pltpu.make_async_remote_copy(
+            src_ref=source.at[to, pl.ds(0, rows)],
+            dst_ref=target.at[me, pl.ds(0, rows)],
+            send_sem=sems[0].at[to],
+            recv_sem=sems[1].at[me],
+            device_id=(to // ny, lax.rem(to, ny)),
+            device_id_type=MESH,
+        )
+
+    places = (cap_rows, send_at, recv_at, (at_send_sem, at_recv_sem))
+    amounts = (3 * cap_rows, send, recv, (send_sem, recv_sem))
+
+    def go_places(s, _):
+        copy_to(s, *places).start()
+        return 0
+
+    lax.fori_loop(1, owners, go_places, 0)
+
+    def pack(row, index, step):
+        mine = own_iota == owner_v[pl.ds(row, 1), :]
         span = pl.ds(pl.multiple_of(step * LANES, LANES), LANES)
-        return [
-            jnp.sum(acc[c].T, axis=0, keepdims=True) * albedo[c : c + 1, span] for c in range(3)
-        ]
-
-    def pack(row, values):
-        mine = own_iota == owner_v[pl.ds(row, 1), :]
         pieces = []
-        for rad in values:
+        for c in range(3):
+            rad = jnp.sum(partial[index, c].T, axis=0, keepdims=True) * albedo[c : c + 1, span]
             high = rad.astype(jnp.bfloat16).astype(jnp.float32)
             pieces += [high, rad - high]
         return jnp.concatenate(
             [jnp.where(mine, v, 0.0).astype(jnp.bfloat16) for v in pieces], axis=0
         )
 
-    def second_half(now, later, was, row, stages, wides, accs):
-        side = pack(row, radiance(was, accs[1]))
+    def second_half(now, later, stages, wides):
         widen(1, later, wides[1])
         for g in range(LANES // ROWS):
             load_group(1, later, g, stages[1])
             here = slice(g * ROWS, (g + 1) * ROWS)
-            totals = sum_group(g, stages[0], wides[0], [partial[now, c, here, :] for c in range(3)])
+            totals = sum_group(
+                g, stages[0], wides[0], [partial[now + 2, c, here, :] for c in range(3)]
+            )
             for c in range(3):
-                accs[0][c, here, :] = totals[c]
-        return side
-
-    def add_packed(sides, pair, width):
-        span = pl.ds(pl.multiple_of(pair * 2 * LANES, LANES), width)
-        packed[...] += lax.dot_general(
-            jnp.concatenate(sides, axis=1), right_v[:, span], NT, preferred_element_type=jnp.float32
-        )
+                partial[now + 2, c, here, :] = totals[c]
 
     def second_two(i, _):
         n = 2 * i
-        side_a = second_half(
-            n, n + 1, jnp.maximum(n - 1, 0), n + ROWS - 1,
-            (stage_a, stage_b), (wide_a, wide_b), (acc_a, acc_b),
-        )
-        side_b = second_half(
-            n + 1, jnp.minimum(n + 2, steps - 1), n, n + ROWS,
-            (stage_b, stage_a), (wide_b, wide_a), (acc_b, acc_a),
-        )
-        add_packed([side_a, side_b], i, 2 * LANES)
+        span = pl.ds(pl.multiple_of(jnp.maximum(n - 4, 0) * LANES, LANES), 2 * LANES)
+        packed[...] += lax.dot_general(
+            side_v[...], right_v[:, span], NT, preferred_element_type=jnp.float32
+        )
+        for u in range(2):
+            side_v[:, u * LANES : (u + 1) * LANES] = pack(n + u, n + u, jnp.maximum(n - 2, 0) + u)
+        second_half(n, n + 1, (stage_a, stage_b), (wide_a, wide_b))
+        second_half(n + 1, jnp.minimum(n + 2, steps - 1), (stage_b, stage_a), (wide_b, wide_a))
         return 0
 
     widen(1, 0, wide_a)
     for g in range(LANES // ROWS):
         load_group(1, 0, g, stage_a)
     lax.fori_loop(0, steps // 2, second_two, 0)
-    add_packed([pack(steps + ROWS - 1, radiance(steps - 1, acc_b))], steps // 2, LANES)
+    sides = [side_v[...]] + [pack(steps + u, steps + u, steps - 2 + u) for u in range(2)]
+    packed[...] += lax.dot_general(
+        jnp.concatenate(sides, axis=1), right_v[:, (steps - 4) * LANES :], NT,
+        preferred_element_type=jnp.float32,
+    )
 
     flat_send = send.reshape(owners * pitch, LANES)
 
@@ -361,28 +373,14 @@
             flat_send[pl.ds(c * cap_rows + j, owners, stride=pitch), :] = (
                 part(2 * c, j) + part(2 * c + 1, j)
             )
-        flat_send[pl.ds(3 * cap_rows + j, owners, stride=pitch), :] = (
-            packed_at[0:owners, j * LANES : (j + 1) * LANES] * float(LANES)
-            + packed_at[owners : 2 * owners, j * LANES : (j + 1) * LANES]
-        )
-
-    def copy_to(s):
-        to = lax.rem(me + s, owners)
-        return pltpu.make_async_remote_copy(
-            src_ref=send.at[to, pl.ds(0, used)],
-            dst_ref=recv.at[me, pl.ds(0, used)],
-            send_sem=send_sem.at[to],
-            recv_sem=recv_sem.at[me],
-            device_id=(to // ny, lax.rem(to, ny)),
-            device_id_type=MESH,
-        )
 
     def go(s, _):
-        copy_to(s).start()
+        copy_to(s, *amounts).start()
         return 0
 
     lax.fori_loop(1, owners, go, 0)
     recv[me] = send[me]
+    recv_at[me] = send_at[me]
 
     halves = out.shape[2] // LANES
     high_rows = tiles_dev * halves
@@ -394,14 +392,15 @@
 
         @pl.when(s > 0)
         def _():
-            pltpu.make_async_remote_copy(
-                src_ref=send.at[come, pl.ds(0, used)],
-                dst_ref=recv.at[come, pl.ds(0, used)],
-                send_sem=send_sem.at[come],
-                recv_sem=recv_sem.at[come],
-                device_id=(come // ny, lax.rem(come, ny)),
-                device_id_type=MESH,
-            ).wait_recv()
+            for rows, source, target, sems in (places, amounts):
+                pltpu.make_async_remote_copy(
+                    src_ref=source.at[come, pl.ds(0, rows)],
+                    dst_ref=target.at[come, pl.ds(0, rows)],
+                    send_sem=sems[0].at[come],
+                    recv_sem=sems[1].at[come],
+                    device_id=(come // ny, lax.rem(come, ny)),
+                    device_id_type=MESH,
+                ).wait_recv()
 
         return come
 
@@ -409,13 +408,13 @@
         lefts, rights = [], []
         sources = [arrive(step * 4 + u) for u in range(4)]
         for come in sources:
-            blk = recv[come]
+            blk, spots = recv[come], recv_at[come]
             for j in range(cap_rows):
                 def row(v):
                     r = v * cap_rows + j
                     return blk[r : r + 1]
 
-                where = row(3)
+                where = spots[j : j + 1]
                 high = jnp.floor(where * (1.0 / LANES))
                 here = high_iota == high
                 pieces = []
@@ -440,7 +439,8 @@
             )
 
     def sent(s, _):
-        copy_to(s).wait_send()
+        copy_to(s, *places).wait_send()
+        copy_to(s, *amounts).wait_send()
         return 0
 
     lax.fori_loop(1, owners, sent, 0)
@@ -456,7 +456,7 @@
     tiles = tile_slot.shape[0]
     tiles_dev = tiles // owners
     cap_rows = -(-(3 * points // owners) // LANES)
-    pitch = -(-4 * cap_rows // ROWS) * ROWS
+    pitch = -(-3 * cap_rows // ROWS) * ROWS
     hb, vm = pl.BlockSpec(memory_space=pl.ANY), pl.BlockSpec(memory_space=pltpu.VMEM)
     dma, f32, i32, bf16 = pltpu.SemaphoreType.DMA, jnp.float32, jnp.int32, jnp.bfloat16
     stage_rows = LANES // ROWS * GROUP
@@ -474,9 +474,8 @@
             pltpu.VMEM((stage_rows, LANES), f32),
             pltpu.VMEM((LANES, 3 * LANES), f32),
             pltpu.VMEM((LANES, 3 * LANES), f32),
-            pltpu.VMEM((3, LANES, LANES), f32),
-            pltpu.VMEM((3, LANES, LANES), f32),
-            pltpu.VMEM((steps, 3, LANES, LANES), f32),
+            pltpu.VMEM((6 * owners, 2 * LANES), bf16),
+            pltpu.VMEM((steps + 2, 3, LANES, LANES), f32),
             pltpu.VMEM((2, 3 * ROWS, 3 * LANES), bf16),
             pltpu.VMEM((LANES, LANES), bf16),
             pltpu.VMEM((cy, cx), i32),
@@ -491,18 +490,21 @@
             pltpu.VMEM((2 * steps, LANES), i32),
             pltpu.SMEM((2 * steps, LANES), i32),
             pltpu.VMEM((steps + ROWS, LANES), i32),
-            pltpu.VMEM((2 * owners, points + 2 * LANES), bf16),
-            pltpu.VMEM((cap_rows * LANES, points + 2 * LANES), bf16),
+            pltpu.VMEM((2 * owners, points), bf16),
+            pltpu.VMEM((cap_rows * LANES, points), bf16),
             pltpu.VMEM((6 * owners, cap_rows * LANES), f32),
-            pltpu.VMEM((2 * owners, cap_rows * LANES), f32),
             pltpu.VMEM((owners, pitch, LANES), f32),
             pltpu.VMEM((owners, pitch, LANES), f32),
+            pltpu.VMEM((owners, ROWS, LANES), f32),
+            pltpu.VMEM((owners, ROWS, LANES), f32),
             dma((CHANNELS,)),
             dma((4 * CHANNELS,)),
             dma((6,)),
             dma,
             dma((8,)),
             dma((8,)),
+            dma((owners,)),
+            dma((owners,)),
             dma((owners,)),
             dma((owners,)),
         ],

time: 38.7 us -> 39.7 us (1.026)
  Pallas kernels: 37.2 us -> 38.2 us
    pallas_call x1, Pallas kernels: 37.2 us -> 38.2 us  [per_device(): pl.pallas_call(functools.partial(whole_kernel, nx, ny, cap_rows, tiles_de...]
where the time goes in v3:
time: 39.7 us; the launch traced here: 39.5 us
  Pallas kernels  38.2 us (96%)
  local copies, waits for them, and re-layouts  1.35 us (3%)
    pallas_call x1, Pallas kernels, per_device(): pl.pallas_call(functools.partial(whole_kernel, nx, ny, cap_rows, tiles_de...  38.2 us
    unnamed x1, local copies, waits for them, and re-layouts  1.35 us

profile of v3, /device:TPU:0, one launch (start us, length us, event | category | flops | bytes accessed | tf_op | source)
XLA Modules:
  0.0 39.5 jit_solution(18276909879929804949)
XLA Ops:
  0.0 38.2 %estimate.1 = f32[3,8,256]{2,1,0:T(8,128)} custom-call(f32[6,64,32,128]{3,2,1,0:T(8,128)} %photons.1, s32[32,64]{1,0:T(8,128)} %bitcast.2, f32[3,4096]{1,0:T(4,128)} %offsets_h.1, s32[4,4096]{1,0:T(4,128)} %blocks_h.1, f32[3,4096]{1,0:T(4,128)} %albedo_h.1, s32[32,128]{1,0:T(8,128)} %bitcast.3, s32[256]{0:T(256)} %tile_slot_h.1), custom_call_target="tpu_custom_call" | custom-call | tf_op jit(solution)/shard_map/estimate/pallas_call | solution.py:463
  38.2 1.3 %copy.9 = f32[3,8,256]{2,1,0:T(8,128)} copy(f32[3,8,256]{2,1,0:T(8,128)} %estimate.1) | data formatting | bytes 49152

commit v4 on v3

--- a/solution.py
+++ b/solution.py
@@ -31,7 +31,7 @@
     table, edge_x, edge_y, ring_y, stage_a, stage_b, wide_a, wide_b, side_v, partial,
     spread, tri, counts, offsets, blocks, albedo, pixels, tile_slot,
     count_row, count_col, points_v, base_v, base_s, owner_v, left_v, right_v,
-    packed, send, recv, send_at, recv_at,
+    packed, send, recv, send_at, recv_at, high_v, low_v,
     fill_sem, edge_sem, small_sem, base_sem, halo_send, halo_recv, send_sem, recv_sem,
     at_send_sem, at_recv_sem,
 ):
@@ -47,14 +47,12 @@
 
     barrier = pltpu.get_barrier_semaphore()
 
-    def greet(s, _):
-        to = lax.rem(me + s, owners)
-        pl.semaphore_signal(
-            barrier, inc=1, device_id=(to // ny, lax.rem(to, ny)), device_id_type=MESH
-        )
-        return 0
-
-    lax.fori_loop(1, owners, greet, 0)
+    def peer(s):
+        to = split_by(me + s, owners)[1]
+        return to, split_by(to, ny)
+
+    for s in range(1, owners):
+        pl.semaphore_signal(barrier, inc=1, device_id=peer(s)[1], device_id_type=MESH)
 
     small = [
         pltpu.make_async_copy(src, dst, small_sem.at[n])
@@ -90,8 +88,20 @@
         edge.start()
     for copy in small[1:]:
         copy.start()
-    for fill in fills:
-        fill.start()
+    a = lax.broadcasted_iota(jnp.int32, (LANES, LANES), 0)
+    b = lax.broadcasted_iota(jnp.int32, (LANES, LANES), 1)
+    tri[...] = jnp.where(a < b, 1.0, 0.0).astype(jnp.bfloat16)
+    for n, rows in enumerate(((0, 1, 2), (0, 3, 2))):
+        a = lax.broadcasted_iota(jnp.int32, spread.shape[1:], 0) % ROWS
+        b = lax.broadcasted_iota(jnp.int32, spread.shape[1:], 1) // LANES
+        hit = (a == rows[0]) & (b == 0)
+        for m in range(1, 3):
+            hit = hit | ((a == rows[m]) & (b == m))
+        spread[n] = jnp.where(hit, 1.0, 0.0).astype(jnp.bfloat16)
+    packed[...] = jnp.zeros_like(packed)
+    side_v[...] = jnp.zeros_like(side_v)
+    points_v[...] = jnp.zeros_like(points_v)
+    owner_v[...] = jnp.full(owner_v.shape, -1, jnp.int32)
 
     small[0].wait()
     count_row[...] = counts[...].astype(jnp.float32)
@@ -110,6 +120,8 @@
 
     for edge in edges:
         edge.wait()
+    for fill in fills:
+        fill.start()
     flat_x = edge_x.reshape(2 * cy * ROWS, LANES)
     flat_y = edge_y.reshape(2 * cx * ROWS, LANES)
     for s, y in enumerate((cy - 1, 0)):
@@ -165,7 +177,6 @@
             base_v[n * steps + j : n * steps + j + 1, :] = bases[n][:, j * LANES : (j + 1) * LANES]
     to_scalar = pltpu.make_async_copy(base_v, base_s, base_sem)
     to_scalar.start()
-    points_v[...] = jnp.zeros_like(points_v)
     points_v[0:1, :] = offsets[0:1, :] + (lx[0:1] - low_x).astype(jnp.float32)
     points_v[1:2, :] = offsets[1:2, :]
     points_v[2:3, :] = offsets[2:3, :]
@@ -184,21 +195,7 @@
     owner, place = split_by(slot, tiles_dev)
     half, low = split_by(within, LANES)
     first = half * tiles_dev + place
-    owner_v[...] = jnp.full(owner_v.shape, -1, jnp.int32)
     owner_v[2 : 2 + steps, :] = owner
-
-    a = lax.broadcasted_iota(jnp.int32, (LANES, LANES), 0)
-    b = lax.broadcasted_iota(jnp.int32, (LANES, LANES), 1)
-    tri[...] = jnp.where(a < b, 1.0, 0.0).astype(jnp.bfloat16)
-    for n, rows in enumerate(((0, 1, 2), (0, 3, 2))):
-        a = lax.broadcasted_iota(jnp.int32, spread.shape[1:], 0) % ROWS
-        b = lax.broadcasted_iota(jnp.int32, spread.shape[1:], 1) // LANES
-        hit = (a == rows[0]) & (b == 0)
-        for m in range(1, 3):
-            hit = hit | ((a == rows[m]) & (b == m))
-        spread[n] = jnp.where(hit, 1.0, 0.0).astype(jnp.bfloat16)
-    packed[...] = jnp.zeros_like(packed)
-    side_v[...] = jnp.zeros_like(side_v)
 
     own_iota = lax.broadcasted_iota(jnp.int32, (owners, LANES), 0)
     cap_iota = lax.broadcasted_iota(jnp.int32, (cap_rows * LANES, LANES), 0).astype(jnp.float32)
@@ -298,25 +295,26 @@
         for x in range(cx + 2):
             table[x, y] = ring_y[s, x]
 
-    def copy_to(s, rows, source, target, sems):
-        to = lax.rem(me + s, owners)
+    def exchange(s, rows, source, target, send_at_sem, recv_at_sem):
+        to, where = peer(s)
         return pltpu.make_async_remote_copy(
             src_ref=source.at[to, pl.ds(0, rows)],
-            dst_ref=target.at[me, pl.ds(0, rows)],
-            send_sem=sems[0].at[to],
-            recv_sem=sems[1].at[me],
-            device_id=(to // ny, lax.rem(to, ny)),
+            dst_ref=target.at[s, pl.ds(0, rows)],
+            send_sem=send_at_sem,
+            recv_sem=recv_at_sem,
+            device_id=where,
             device_id_type=MESH,
         )
 
-    places = (cap_rows, send_at, recv_at, (at_send_sem, at_recv_sem))
-    amounts = (3 * cap_rows, send, recv, (send_sem, recv_sem))
-
-    def go_places(s, _):
-        copy_to(s, *places).start()
-        return 0
-
-    lax.fori_loop(1, owners, go_places, 0)
+    def several(start, count, rows, target, send_at_sem, recv_at_sem):
+        part = target.at[pl.ds(start, count), pl.ds(0, rows)]
+        return pltpu.make_async_remote_copy(
+            src_ref=part, dst_ref=part, send_sem=send_at_sem, recv_sem=recv_at_sem,
+            device_id=peer(1)[1], device_id_type=MESH,
+        )
+
+    for s in range(1, owners):
+        exchange(s, cap_rows, send_at, recv_at, at_send_sem, at_recv_sem).start()
 
     def pack(row, index, step):
         mine = own_iota == owner_v[pl.ds(row, 1), :]
@@ -374,63 +372,57 @@
                 part(2 * c, j) + part(2 * c + 1, j)
             )
 
-    def go(s, _):
-        copy_to(s, *amounts).start()
-        return 0
-
-    lax.fori_loop(1, owners, go, 0)
-    recv[me] = send[me]
-    recv_at[me] = send_at[me]
+    for s in range(1, owners):
+        exchange(s, 3 * cap_rows, send, recv, send_sem, recv_sem.at[s // 4]).start()
+    recv[0] = send[me]
+    recv_at[0] = send_at[me]
+    everyone = several(1, owners - 1, cap_rows, recv_at, at_send_sem, at_recv_sem)
+    everyone.wait_recv()
 
     halves = out.shape[2] // LANES
     high_rows = tiles_dev * halves
     high_iota = lax.broadcasted_iota(jnp.int32, (high_rows, LANES), 0).astype(jnp.float32)
     low_iota = lax.broadcasted_iota(jnp.int32, (LANES, LANES), 0).astype(jnp.float32)
 
-    def arrive(s):
-        come = lax.rem(me + owners - s, owners)
-
-        @pl.when(s > 0)
-        def _():
-            for rows, source, target, sems in (places, amounts):
-                pltpu.make_async_remote_copy(
-                    src_ref=source.at[come, pl.ds(0, rows)],
-                    dst_ref=target.at[come, pl.ds(0, rows)],
-                    send_sem=sems[0].at[come],
-                    recv_sem=sems[1].at[come],
-                    device_id=(come // ny, lax.rem(come, ny)),
-                    device_id_type=MESH,
-                ).wait_recv()
-
-        return come
-
-    def add(step, total):
-        lefts, rights = [], []
-        sources = [arrive(step * 4 + u) for u in range(4)]
-        for come in sources:
-            blk, spots = recv[come], recv_at[come]
+    def spots(q, _):
+        rights = []
+        for u in range(4):
+            blk = recv_at[q * 4 + u]
             for j in range(cap_rows):
-                def row(v):
-                    r = v * cap_rows + j
-                    return blk[r : r + 1]
-
-                where = spots[j : j + 1]
+                where = blk[j : j + 1]
                 high = jnp.floor(where * (1.0 / LANES))
-                here = high_iota == high
+                at = (q * 4 + u) * ROWS + j
+                high_v[pl.ds(at, 1), :] = high
+                rights.append(
+                    jnp.where(low_iota == where - high * float(LANES), 1.0, 0.0).astype(jnp.bfloat16)
+                )
+        low_v[q] = jnp.concatenate(rights, axis=1)
+        return 0
+
+    lax.fori_loop(0, owners // 4, spots, 0)
+
+    def add(q, total):
+        lefts = []
+        for u in range(4):
+            blk = recv[q * 4 + u]
+            for j in range(cap_rows):
+                here = high_iota == high_v[pl.ds((q * 4 + u) * ROWS + j, 1), :]
                 pieces = []
                 for c in range(3):
-                    value = row(c)
+                    value = blk[c * cap_rows + j : c * cap_rows + j + 1]
                     top = value.astype(jnp.bfloat16).astype(jnp.float32)
                     pieces += [jnp.where(here, top, 0.0), jnp.where(here, value - top, 0.0)]
                 lefts.append(jnp.concatenate(pieces, axis=0).astype(jnp.bfloat16))
-                rights.append(
-                    jnp.where(low_iota == where - high * float(LANES), 1.0, 0.0).astype(jnp.bfloat16)
-                )
         left = jnp.concatenate(lefts, axis=1)
-        right = jnp.concatenate(rights, axis=1)
-        return total + lax.dot_general(left, right, NT, preferred_element_type=jnp.float32)
-
-    total = lax.fori_loop(0, owners // 4, add, jnp.zeros((6 * high_rows, LANES), jnp.float32))
+        return total + lax.dot_general(left, low_v[q], NT, preferred_element_type=jnp.float32)
+
+    def wait_add(q, total):
+        several(q * 4, 4, 3 * cap_rows, recv, send_sem, recv_sem.at[q]).wait_recv()
+        return add(q, total)
+
+    several(1, 3, 3 * cap_rows, recv, send_sem, recv_sem.at[0]).wait_recv()
+    total = add(0, jnp.zeros((6 * high_rows, LANES), jnp.float32))
+    total = lax.fori_loop(1, owners // 4, wait_add, total)
     for c in range(3):
         for h in range(halves):
             at = 2 * c * high_rows + h * tiles_dev
@@ -438,12 +430,8 @@
                 total[at : at + tiles_dev] + total[at + high_rows : at + high_rows + tiles_dev]
             )
 
-    def sent(s, _):
-        copy_to(s, *places).wait_send()
-        copy_to(s, *amounts).wait_send()
-        return 0
-
-    lax.fori_loop(1, owners, sent, 0)
+    everyone.wait_send()
+    several(1, owners - 1, 3 * cap_rows, recv, send_sem, recv_sem.at[0]).wait_send()
 
 
 def per_device(
@@ -497,16 +485,18 @@
             pltpu.VMEM((owners, pitch, LANES), f32),
             pltpu.VMEM((owners, ROWS, LANES), f32),
             pltpu.VMEM((owners, ROWS, LANES), f32),
+            pltpu.VMEM((owners * ROWS, LANES), f32),
+            pltpu.VMEM((owners // 4, LANES, 4 * cap_rows * LANES), bf16),
             dma((CHANNELS,)),
             dma((4 * CHANNELS,)),
             dma((6,)),
             dma,
             dma((8,)),
             dma((8,)),
-            dma((owners,)),
-            dma((owners,)),
-            dma((owners,)),
-            dma((owners,)),
+            dma,
+            dma((owners // 4,)),
+            dma,
+            dma,
         ],
         compiler_params=pltpu.CompilerParams(collective_id=0, has_side_effects=True),
         name="estimate",

time: 39.7 us -> 37.6 us (0.947)
  Pallas kernels: 38.2 us -> 36 us
    pallas_call x1, Pallas kernels: 38.2 us -> 36 us  [per_device(): pl.pallas_call(functools.partial(whole_kernel, nx, ny, cap_rows, tiles_de...]
where the time goes in v4:
time: 37.6 us; the launch traced here: 37.4 us
  Pallas kernels  36 us (96%)
  local copies, waits for them, and re-layouts  1.35 us (4%)
    pallas_call x1, Pallas kernels, per_device(): pl.pallas_call(functools.partial(whole_kernel, nx, ny, cap_rows, tiles_de...  36 us
    unnamed x1, local copies, waits for them, and re-layouts  1.35 us

profile of v4, /device:TPU:0, one launch (start us, length us, event | category | flops | bytes accessed | tf_op | source)
XLA Modules:
  0.0 37.4 jit_solution(195610938064107427)
XLA Ops:
  0.0 36.0 %estimate.1 = f32[3,8,256]{2,1,0:T(8,128)} custom-call(f32[6,64,32,128]{3,2,1,0:T(8,128)} %photons.1, s32[32,64]{1,0:T(8,128)} %bitcast.2, f32[3,4096]{1,0:T(4,128)} %offsets_h.1, s32[4,4096]{1,0:T(4,128)} %blocks_h.1, f32[3,4096]{1,0:T(4,128)} %albedo_h.1, s32[32,128]{1,0:T(8,128)} %bitcast.3, s32[256]{0:T(256)} %tile_slot_h.1), custom_call_target="tpu_custom_call" | custom-call | tf_op jit(solution)/shard_map/estimate/pallas_call | solution.py:451
  36.0 1.3 %copy.9 = f32[3,8,256]{2,1,0:T(8,128)} copy(f32[3,8,256]{2,1,0:T(8,128)} %estimate.1) | data formatting | bytes 49152
